TPU v7x, 32 devices: a whole 2x2x4 slice. The times are simulated.
32 devices in a mesh: lat: 4 (over z), rad: 8 (over y, x, core).
Axes of the slice: x: 2, y: 2, z: 4, core: 2. Of those that a mesh axis runs over, the one named last changes fastest.
Arguments:
- positions: float32 [4096, 3, 128], P(('lat', 'rad')), may hold values from 0 to 1
- fields: bfloat16 [4096, 16, 128], P(('lat', 'rad')), may hold values from -6 to 6
- velocity: float32 [81, 8192], P(None, ('lat', 'rad')), may hold values from -3 to 3
- counts: int32 [32], P(('lat', 'rad')), may hold values from 1 to 128, as said below
- elements: int32 [3, 4096], P(None, ('lat', 'rad')), may hold values from 0 to 255
- routes: int32 [2, 4096], P(None, ('lat', 'rad')), may hold values from 0 to 239
Outputs:
- moved: float32 [7680, 3, 128], P(('lat', 'rad'))
- projected: float32 [27, 16, 8192], P(None, None, ('lat', 'rad'))
Inputs may be any that keep to these rules, and one draw needn't show every extreme that they name: counts[d] is at most 128 and equals 128 on some device.
All inputs are finite; a program needn't handle non-finite values.
Results may differ from a plain program's by a relative error of at most 0.0003.
Values sent between devices are 32-bit elements; how exact they have to be, the bound alone decides.
No kernel may reach another device: no remote copies, remote signals or barrier semaphores. Data moves between devices by JAX's collectives and lax.ppermute only.
A program may use at most 64 MiB of HBM per device.

v0:
```python
import jax
import jax.numpy as jnp
from jax import lax
from jax.sharding import PartitionSpec as P

time_step = 0.4
exact = lax.Precision.HIGHEST


def passed_along(x, axis, by):
    size = lax.axis_size(axis)
    return lax.ppermute(x, axis, [(i, (i + by) % size) for i in range(size)])


def lagrange(coord):
    first_node = 2.0 * (coord - 0.5) * (coord - 1.0)
    middle_node = -4.0 * coord * (coord - 1.0)
    last_node = 2.0 * coord * (coord - 0.5)
    return jnp.stack([first_node, middle_node, last_node], axis=0)


def basis(points):
    along_x = lagrange(points[:, 0, :])
    along_y = lagrange(points[:, 1, :])
    along_z = lagrange(points[:, 2, :])
    table = along_x[:, None, None] * along_y[None, :, None] * along_z[None, None, :]
    return jnp.moveaxis(table.reshape(27, points.shape[0], points.shape[2]), 0, 1)


def speed(columns, points):
    coefficients = columns.T.reshape(points.shape[0], 3, 27)
    return jnp.einsum("scn,snb->scb", coefficients, basis(points), precision=exact)


def place_rows(target, valid, number):
    matches = (target[:, None] == jnp.arange(number, dtype=jnp.int32)[None, :]) & valid[:, None]
    present = jnp.any(matches, axis=0)
    source = jnp.sum(
        jnp.where(matches, jnp.arange(target.shape[0], dtype=jnp.int32)[:, None], 0), axis=0
    )
    return (source, present)


def arrange(cargo, source, present):
    result = []
    for member in cargo:
        picked = jnp.take(member, source, axis=0)
        layout = (present.shape[0],) + (1,) * (member.ndim - 1)
        result.append(jnp.where(present.reshape(layout), picked, jnp.zeros_like(picked)))
    return tuple(result)


def migrate(cargo, rad_count, capacity):
    kinds = tuple((member.dtype for member in cargo))
    shaped = tuple(
        (
            member.astype(jnp.float32).reshape((3, rad_count, capacity) + member.shape[1:])
            for member in cargo
        )
    )
    crossed = lax.all_to_all(shaped, "rad", split_axis=1, concat_axis=1, tiled=True)
    sheets = []
    for sheet_number in range(3):
        portion = tuple((member[sheet_number] for member in crossed))
        if sheet_number != 1:
            portion = passed_along(portion, "lat", sheet_number - 1)
        sheets.append(portion)
    moved = tuple(
        (
            jnp.stack([sheets[sheet_number][member_index] for sheet_number in range(3)])
            for member_index in range(len(cargo))
        )
    )
    result = []
    for member, kind in zip(moved, kinds):
        flat = member.reshape((3 * rad_count * capacity,) + member.shape[3:])
        result.append(flat.astype(jnp.int32) if kind == jnp.int32 else flat)
    return tuple(result)


def block_sums(points, carried):
    shapes = basis(points)
    moments = jnp.einsum("snb,sfb->snf", shapes, carried, precision=exact)
    return (moments, jnp.sum(shapes * shapes, axis=2))


def per_device(positions, fields, velocity, counts, elements, routes):
    rad_count = lax.axis_size("rad")
    blocks = positions.shape[0]
    capacity = max(1, 2 * blocks // (3 * rad_count))
    places = 3 * rad_count * capacity
    owned = velocity.shape[1]
    home_valid = jnp.arange(blocks, dtype=jnp.int32) < counts[0]
    first_speed = speed(jnp.take(velocity, elements[0], axis=1), positions)
    midway = positions + 0.5 * time_step * first_speed
    source, present = place_rows(routes[0], home_valid, places)
    wide_fields = fields.astype(jnp.float32)
    labels = jnp.stack([home_valid.astype(jnp.int32), elements[1], routes[1], elements[2]], axis=1)
    pairs = jnp.stack([positions, midway], axis=1)
    labels, pairs, carried = migrate(
        arrange((labels, pairs, wide_fields), source, present), rad_count, capacity
    )
    mid_valid = labels[:, 0] > 0
    second_speed = speed(jnp.take(velocity, labels[:, 1], axis=1), pairs[:, 1])
    landed = pairs[:, 0] + time_step * second_speed
    source, present = place_rows(labels[:, 2], mid_valid, places)
    tags = jnp.stack([mid_valid.astype(jnp.int32), labels[:, 3]], axis=1)
    moments, weights_sum = block_sums(landed, carried)
    tags, arrived, moments, weights_sum = migrate(
        arrange((tags, landed, moments, weights_sum), source, present), rad_count, capacity
    )
    final_valid = tags[:, 0] > 0
    hits = (
        (tags[:, 1][:, None] == jnp.arange(owned, dtype=jnp.int32)[None, :]) & final_valid[:, None]
    ).astype(jnp.float32)
    totals = jnp.einsum("se,snf->nfe", hits, moments, precision=exact)
    weights = jnp.einsum("se,sn->ne", hits, weights_sum, precision=exact)
    projected = totals / (1.0 + weights[:, None, :])
    return (arrived, projected)


def solution(mesh):
    in_specs = (
        P(("lat", "rad"), None, None),
        P(("lat", "rad"), None, None),
        P(None, ("lat", "rad")),
        P(("lat", "rad")),
        P(None, ("lat", "rad")),
        P(None, ("lat", "rad")),
    )
    out_specs = (P(("lat", "rad"), None, None), P(None, None, ("lat", "rad")))
    return jax.shard_map(
        per_device, mesh=mesh, in_specs=in_specs, out_specs=out_specs, check_vma=False
    )
```

profile of v0, /device:TPU:0, one launch (start us, length us, event | category | flops | bytes accessed | tf_op | source)
XLA Modules:
  0.0 182.4 jit_solution(13250675665100041835)
XLA Ops:
  4.3 5.2 %all-to-all-start = ((f32[3,8,10,4]{2,3,0,1:T(4,128)}), f32[3,8,10,4]{2,3,0,1:T(4,128)S(1)}, u32[]{:S(2)}, u32[]{:S(2)}) async-start(f32[3,8,10,4]{2,3,0,1:T(4,128)} %copy.368), calls=%async_computation | async-start | bytes 98304 | tf_op jit(solution)/shard_map/all_to_all | solution.py:61
  13.1 2.7 %fusion.13 = f32[128,1,3,128]{3,2,0,1:T(4,128)S(1)} fusion(f32[128,3,27]{2,1,0:T(4,128)S(1)} %reshape.932, f32[128,27,128]{2,0,1:T(8,128)S(1)} %bitcast.202, f32[128,3,128]{2,0,1:T(8,128)S(1)} %copy-done), kind=kOutput, calls=%fused_computation.26 | convolution fusion | flops 16023552 | bytes 2204160 | tf_op jit(solution)/shard_map/scn,snb->scb/dot_general | solution.py:32
  17.7 2.2 %collective-permute-start = (f32[8,10,4]{1,0,2:T(8,128)S(1)}, f32[8,10,4]{1,0,2:T(8,128)S(1)}, u32[]{:S(2)}, u32[]{:S(2)}) collective-permute-start(f32[8,10,4]{1,0,2:T(8,128)S(1)} %bitcast.225), channel_id=1, source_target_pairs={{0,24},{8,0},{16,8},{24,16},{1,25},{9,1},{17,9},{25,17},{2,26},{10... | collective-permute-start | bytes 3848 | tf_op jit(solution)/shard_map/ppermute | solution.py:12
  24.1 4.2 %all-to-all-start.5 = ((f32[3,8,10,2]{2,3,0,1:T(2,128)}), f32[3,8,10,2]{2,3,0,1:T(2,128)S(1)}, u32[]{:S(2)}, u32[]{:S(2)}) async-start(f32[3,8,10,2]{2,3,0,1:T(2,128)} %copy.408), calls=%async_computation.5 | async-start | bytes 49152 | tf_op jit(solution)/shard_map/all_to_all | solution.py:61
  28.2 1.9 %fusion.16 = f32[3,8,10,2,3,128]{5,3,4,2,0,1:T(2,128)} fusion(f32[3,8,10,2,3,128]{5,4,3,2,1,0:T(4,128)S(1)} %bitcast.207, pred[3,8,10]{2,0,1:T(4,128)(4,1)S(1)} %copy.374, pred[3,8,10]{2,0,1:T(4,128)(4,1)S(1)} %copy.373), kind=kLoop, calls=%fused_computation.31 | loop fusion | flops 368640 | bytes 1475040 | tf_op jit(solution)/shard_map/jit(_where)/select_n | solution.py:49
  33.0 3.5 %all-to-all-start.1 = ((f32[3,8,10,2,3,128]{5,3,4,2,0,1:T(2,128)}), f32[3,8,10,2,3,128]{5,3,4,2,0,1:T(2,128)S(1)}, u32[]{:S(2)}, u32[]{:S(2)}) async-start(f32[3,8,10,2,3,128]{5,3,4,2,0,1:T(2,128)} %fusion.16), calls=%async_computation.1 | async-start | bytes 1474560 | tf_op jit(solution)/shard_map/all_to_all | solution.py:61
  40.9 2.5 %collective-permute-start.10 = (f32[8,10,2]{1,0,2:T(8,128)S(1)}, f32[8,10,2]{1,0,2:T(8,128)S(1)}, u32[]{:S(2)}, u32[]{:S(2)}) collective-permute-start(f32[8,10,2]{1,0,2:T(8,128)S(1)} %bitcast.233), channel_id=1, source_target_pairs={{0,24},{8,0},{16,8},{24,16},{1,25},{9,1},{17,9},{25,17},{2,26},{10... | collective-permute-start | bytes 1928 | tf_op jit(solution)/shard_map/ppermute | solution.py:12
  43.4 5.1 %all-to-all-done.1 = f32[3,8,10,2,3,128]{5,3,4,2,0,1:T(2,128)S(1)} async-done(((f32[3,8,10,2,3,128]{5,3,4,2,0,1:T(2,128)}), f32[3,8,10,2,3,128]{5,3,4,2,0,1:T(2,128)S(1)}, u32[]{:S(2)}, u32[]{:S(2)}) %all-to-all-start.1) | async-done | bytes 737312 | tf_op jit(solution)/shard_map/all_to_all | solution.py:61
  48.5 4.3 %all-to-all-start.3 = ((f32[3,8,10,16,128]{4,3,2,0,1:T(8,128)}), f32[3,8,10,16,128]{4,3,2,0,1:T(8,128)}, u32[]{:S(2)}, u32[]{:S(2)}) async-start(f32[3,8,10,16,128]{4,3,2,0,1:T(8,128)} %copy.399), calls=%async_computation.3 | async-start | bytes 3932160 | tf_op jit(solution)/shard_map/all_to_all | solution.py:61
  53.1 3.9 %collective-permute-start.2 = (f32[8,10,2,3,128]{4,2,3,1,0:T(2,128)S(1)}, f32[8,10,2,3,128]{4,2,3,1,0:T(2,128)S(1)}, u32[]{:S(2)}, u32[]{:S(2)}) collective-permute-start(f32[8,10,2,3,128]{4,2,3,1,0:T(2,128)S(1)} %get-tuple-element.12), channel_id=1, source_target_pairs={{0,24},{8,0},{16,8},{24,16},{1,25},{9,1},{17,9},{25,17},{2,26},{10... | collective-permute-start | bytes 737288 | tf_op jit(solution)/shard_map/ppermute | solution.py:12
  57.5 5.9 %collective-permute-done.2 = f32[8,10,2,3,128]{4,2,3,1,0:T(2,128)S(1)} collective-permute-done((f32[8,10,2,3,128]{4,2,3,1,0:T(2,128)S(1)}, f32[8,10,2,3,128]{4,2,3,1,0:T(2,128)S(1)}, u32[]{:S(2)}, u32[]{:S(2)}) %collective-permute-start.2) | collective-permute-done | bytes 245792 | tf_op jit(solution)/shard_map/ppermute | solution.py:12
  63.4 5.4 %collective-permute-done.3 = f32[8,10,2,3,128]{4,2,3,1,0:T(2,128)S(1)} collective-permute-done((f32[8,10,2,3,128]{4,2,3,1,0:T(2,128)S(1)}, f32[8,10,2,3,128]{4,2,3,1,0:T(2,128)S(1)}, u32[]{:S(2)}, u32[]{:S(2)}) %collective-permute-start.3) | collective-permute-done | bytes 245792 | tf_op jit(solution)/shard_map/ppermute | solution.py:12
  70.2 4.1 %fusion.2 = f32[240,3,128]{2,1,0:T(4,128)S(1)} fusion(f32[240,3,27]{2,1,0:T(4,128)S(1)} %reshape.933, f32[240,27,128]{2,0,1:T(8,128)S(1)} %bitcast.201), kind=kOutput, calls=%fused_computation.11 | convolution fusion | flops 29859840 | bytes 3764160 | tf_op jit(solution)/shard_map/scn,snb->scb/dot_general | solution.py:32
  80.2 2.8 %slice_bitcast_fusion.5 = (f32[8,10,16,128]{3,2,1,0:T(8,128)}, f32[8,10,16,128]{3,2,1,0:T(8,128)}, f32[1,8,10,16,128]{4,3,2,1,0:T(8,128)}) fusion(f32[3,8,10,16,128]{4,3,2,0,1:T(8,128)} %all-to-all-done.3), kind=kLoop, calls=%fused_computation.37 | loop fusion | bytes 3932160 | tf_op jit(solution)/shard_map/squeeze | solution.py:64
  83.0 2.0 %collective-permute-start.6 = (f32[8,10,16,128]{3,2,1,0:T(8,128)}, f32[8,10,16,128]{3,2,1,0:T(8,128)}, u32[]{:S(2)}, u32[]{:S(2)}) collective-permute-start(f32[8,10,16,128]{3,2,1,0:T(8,128)} %get-tuple-element.7), channel_id=1, source_target_pairs={{0,24},{8,0},{16,8},{24,16},{1,25},{9,1},{17,9},{25,17},{2,26},{10... | collective-permute-start | bytes 1966088 | tf_op jit(solution)/shard_map/ppermute | solution.py:12
  86.1 3.8 %all-to-all-start.6 = ((f32[8,1,810]{2,1,0:T(1,128)}), f32[8,1,810]{2,1,0:T(1,128)S(1)}, u32[]{:S(2)}, u32[]{:S(2)}) async-start(f32[8,1,810]{2,1,0:T(1,128)} %reshape.939), calls=%async_computation.6 | async-start | bytes 57344 | tf_op jit(solution)/shard_map/all_to_all | solution.py:61
  92.2 2.6 %all-to-all-done.6 = f32[8,1,810]{2,1,0:T(1,128)S(1)} async-done(((f32[8,1,810]{2,1,0:T(1,128)}), f32[8,1,810]{2,1,0:T(1,128)S(1)}, u32[]{:S(2)}, u32[]{:S(2)}) %all-to-all-start.6) | async-done | bytes 25952 | tf_op jit(solution)/shard_map/all_to_all | solution.py:61
  94.7 4.2 %all-to-all-start.2 = ((f32[3,8,10,3,128]{4,3,2,0,1:T(4,128)}), f32[3,8,10,3,128]{4,3,2,0,1:T(4,128)}, u32[]{:S(2)}, u32[]{:S(2)}) async-start(f32[3,8,10,3,128]{4,3,2,0,1:T(4,128)} %copy.393), calls=%async_computation.2 | async-start | bytes 983040 | tf_op jit(solution)/shard_map/all_to_all | solution.py:61
  100.4 1.8 %collective-permute-start.13 = (f32[8,10,27]{2,0,1:T(8,128)S(1)}, f32[8,10,27]{2,0,1:T(8,128)S(1)}, u32[]{:S(2)}, u32[]{:S(2)}) collective-permute-start(f32[8,10,27]{2,0,1:T(8,128)S(1)} %bitcast.222), channel_id=1, source_target_pairs={{0,8},{8,16},{16,24},{24,0},{1,9},{9,17},{17,25},{25,1},{2,10},{10... | collective-permute-start | bytes 25928 | tf_op jit(solution)/shard_map/ppermute | solution.py:12
  102.2 2.3 %collective-permute-start.12 = (f32[8,10,27]{2,0,1:T(8,128)S(1)}, f32[8,10,27]{2,0,1:T(8,128)S(1)}, u32[]{:S(2)}, u32[]{:S(2)}) collective-permute-start(f32[8,10,27]{2,0,1:T(8,128)S(1)} %bitcast.221), channel_id=1, source_target_pairs={{0,24},{8,0},{16,8},{24,16},{1,25},{9,1},{17,9},{25,17},{2,26},{10... | collective-permute-start | bytes 25928 | tf_op jit(solution)/shard_map/ppermute | solution.py:12
  104.5 10.3 %collective-permute-done.7 = f32[8,10,16,128]{3,2,1,0:T(8,128)} collective-permute-done((f32[8,10,16,128]{3,2,1,0:T(8,128)}, f32[8,10,16,128]{3,2,1,0:T(8,128)}, u32[]{:S(2)}, u32[]{:S(2)}) %collective-permute-start.7) | collective-permute-done | bytes 655392 | tf_op jit(solution)/shard_map/ppermute | solution.py:12
  116.5 8.2 %fusion = f32[240,27,16]{1,2,0:T(8,128)} fusion(f32[240,16,128]{2,1,0:T(8,128)S(1)} %bitcast.206, f32[240,27,128]{2,0,1:T(8,128)S(1)} %bitcast.199), kind=kOutput, calls=%fused_computation.9 | convolution fusion | flops 159252480 | bytes 5698560 | tf_op jit(solution)/shard_map/snb,sfb->snf/dot_general | solution.py:83
  124.6 2.3 %gather_fusion.6 = f32[240,27,16]{1,2,0:T(8,128)S(1)} fusion(f32[240,27,16]{1,2,0:T(8,128)} %fusion, s32[1024]{0:T(1024)S(1)} %pad_clamp_fusion), kind=kCustom, calls=%fused_computation.6 | custom fusion | bytes 830400 | tf_op jit(solution)/shard_map/jit(_take)/gather | solution.py:47
  126.9 2.2 %fusion.37 = f32[8,3,10,16,27]{4,3,2,1,0:T(8,128)} fusion(f32[3,8,10,27,16]{3,4,2,1,0:T(8,128)S(1)} %bitcast.200, pred[3,8,10]{2,0,1:T(4,128)(4,1)S(1)} %copy.398, pred[3,8,10]{2,0,1:T(4,128)(4,1)S(1)} %copy.397), kind=kLoop, calls=%fused_computation.153 | loop fusion | flops 207360 | bytes 829920
  129.1 4.0 %reshape.937 = f32[8,1,12960]{2,1,0:T(1,128)} reshape(f32[8,3,10,16,27]{4,3,2,1,0:T(8,128)} %fusion.37) | data formatting | bytes 829440
  133.1 3.6 %all-to-all-start.4 = ((f32[8,1,12960]{2,1,0:T(1,128)}), f32[8,1,12960]{2,1,0:T(1,128)S(1)}, u32[]{:S(2)}, u32[]{:S(2)}) async-start(f32[8,1,12960]{2,1,0:T(1,128)} %reshape.937), calls=%async_computation.4 | async-start | bytes 835584 | tf_op jit(solution)/shard_map/all_to_all | solution.py:61
  138.0 2.0 %collective-permute-start.4 = (f32[8,10,3,128]{3,2,1,0:T(4,128)S(1)}, f32[8,10,3,128]{3,2,1,0:T(4,128)S(1)}, u32[]{:S(2)}, u32[]{:S(2)}) collective-permute-start(f32[8,10,3,128]{3,2,1,0:T(4,128)S(1)} %get-tuple-element.15), channel_id=1, source_target_pairs={{0,24},{8,0},{16,8},{24,16},{1,25},{9,1},{17,9},{25,17},{2,26},{10... | collective-permute-start | bytes 368648 | tf_op jit(solution)/shard_map/ppermute | solution.py:12
  140.1 5.2 %all-to-all-done.4 = f32[8,1,12960]{2,1,0:T(1,128)S(1)} async-done(((f32[8,1,12960]{2,1,0:T(1,128)}), f32[8,1,12960]{2,1,0:T(1,128)S(1)}, u32[]{:S(2)}, u32[]{:S(2)}) %all-to-all-start.4) | async-done | bytes 414752 | tf_op jit(solution)/shard_map/all_to_all | solution.py:61
  146.9 2.0 %reshape.938 = f32[8,3,10,16,27]{4,3,2,1,0:T(8,128)S(1)} reshape(f32[8,12960]{1,0:T(8,128)S(1)} %reduce.6) | data formatting | bytes 829440
  149.1 2.0 %collective-permute-start.8 = (f32[8,10,27,16]{2,3,1,0:T(8,128)S(1)}, f32[8,10,27,16]{2,3,1,0:T(8,128)S(1)}, u32[]{:S(2)}, u32[]{:S(2)}) collective-permute-start(f32[8,10,27,16]{2,3,1,0:T(8,128)S(1)} %get-tuple-element.4), channel_id=1, source_target_pairs={{0,24},{8,0},{16,8},{24,16},{1,25},{9,1},{17,9},{25,17},{2,26},{10... | collective-permute-start | bytes 414728 | tf_op jit(solution)/shard_map/ppermute | solution.py:12
  152.4 13.8 %collective-permute-done.8 = f32[8,10,27,16]{2,3,1,0:T(8,128)S(1)} collective-permute-done((f32[8,10,27,16]{2,3,1,0:T(8,128)S(1)}, f32[8,10,27,16]{2,3,1,0:T(8,128)S(1)}, u32[]{:S(2)}, u32[]{:S(2)}) %collective-permute-start.8) | collective-permute-done | bytes 138272 | tf_op jit(solution)/shard_map/ppermute | solution.py:12
  166.2 13.7 %collective-permute-done.9 = f32[8,10,27,16]{2,3,1,0:T(8,128)S(1)} collective-permute-done((f32[8,10,27,16]{2,3,1,0:T(8,128)S(1)}, f32[8,10,27,16]{2,3,1,0:T(8,128)S(1)}, u32[]{:S(2)}, u32[]{:S(2)}) %collective-permute-start.9) | collective-permute-done | bytes 138272 | tf_op jit(solution)/shard_map/ppermute | solution.py:12
  (145 shorter events, 40.7 us)
Async XLA Ops:
  0.6 12.1 %copy-start = (f32[128,3,128]{2,0,1:T(8,128)S(1)}, f32[128,3,128]{2,0,1:T(8,128)}, u32[]{:S(2)}) copy-start(f32[128,3,128]{2,0,1:T(8,128)} %param.6) | copy-start | bytes 589828
  4.3 11.7 %all-to-all-start = ((f32[3,8,10,4]{2,3,0,1:T(4,128)}), f32[3,8,10,4]{2,3,0,1:T(4,128)S(1)}, u32[]{:S(2)}, u32[]{:S(2)}) async-start(f32[3,8,10,4]{2,3,0,1:T(4,128)} %copy.368), calls=%async_computation | async-start | bytes 98304 | tf_op jit(solution)/shard_map/all_to_all | solution.py:61
  16.0 5.6 %collective-permute-start.1 = (f32[8,10,4]{1,0,2:T(8,128)S(1)}, f32[8,10,4]{1,0,2:T(8,128)S(1)}, u32[]{:S(2)}, u32[]{:S(2)}) collective-permute-start(f32[8,10,4]{1,0,2:T(8,128)S(1)} %bitcast.226), channel_id=1, source_target_pairs={{0,8},{8,16},{16,24},{24,0},{1,9},{9,17},{17,25},{25,1},{2,10},{10... | collective-permute-start | bytes 3848 | tf_op jit(solution)/shard_map/ppermute | solution.py:12
  17.7 4.0 %collective-permute-start = (f32[8,10,4]{1,0,2:T(8,128)S(1)}, f32[8,10,4]{1,0,2:T(8,128)S(1)}, u32[]{:S(2)}, u32[]{:S(2)}) collective-permute-start(f32[8,10,4]{1,0,2:T(8,128)S(1)} %bitcast.225), channel_id=1, source_target_pairs={{0,24},{8,0},{16,8},{24,16},{1,25},{9,1},{17,9},{25,17},{2,26},{10... | collective-permute-start | bytes 3848 | tf_op jit(solution)/shard_map/ppermute | solution.py:12
  24.1 9.0 %all-to-all-start.5 = ((f32[3,8,10,2]{2,3,0,1:T(2,128)}), f32[3,8,10,2]{2,3,0,1:T(2,128)S(1)}, u32[]{:S(2)}, u32[]{:S(2)}) async-start(f32[3,8,10,2]{2,3,0,1:T(2,128)} %copy.408), calls=%async_computation.5 | async-start | bytes 49152 | tf_op jit(solution)/shard_map/all_to_all | solution.py:61
  33.0 15.5 %all-to-all-start.1 = ((f32[3,8,10,2,3,128]{5,3,4,2,0,1:T(2,128)}), f32[3,8,10,2,3,128]{5,3,4,2,0,1:T(2,128)S(1)}, u32[]{:S(2)}, u32[]{:S(2)}) async-start(f32[3,8,10,2,3,128]{5,3,4,2,0,1:T(2,128)} %fusion.16), calls=%async_computation.1 | async-start | bytes 1474560 | tf_op jit(solution)/shard_map/all_to_all | solution.py:61
  39.5 17.9 %collective-permute-start.11 = (f32[8,10,2]{1,0,2:T(8,128)S(1)}, f32[8,10,2]{1,0,2:T(8,128)S(1)}, u32[]{:S(2)}, u32[]{:S(2)}) collective-permute-start(f32[8,10,2]{1,0,2:T(8,128)S(1)} %bitcast.234), channel_id=1, source_target_pairs={{0,8},{8,16},{16,24},{24,0},{1,9},{9,17},{17,25},{25,1},{2,10},{10... | collective-permute-start | bytes 1928 | tf_op jit(solution)/shard_map/ppermute | solution.py:12
  40.9 16.5 %collective-permute-start.10 = (f32[8,10,2]{1,0,2:T(8,128)S(1)}, f32[8,10,2]{1,0,2:T(8,128)S(1)}, u32[]{:S(2)}, u32[]{:S(2)}) collective-permute-start(f32[8,10,2]{1,0,2:T(8,128)S(1)} %bitcast.233), channel_id=1, source_target_pairs={{0,24},{8,0},{16,8},{24,16},{1,25},{9,1},{17,9},{25,17},{2,26},{10... | collective-permute-start | bytes 1928 | tf_op jit(solution)/shard_map/ppermute | solution.py:12
  48.5 31.6 %all-to-all-start.3 = ((f32[3,8,10,16,128]{4,3,2,0,1:T(8,128)}), f32[3,8,10,16,128]{4,3,2,0,1:T(8,128)}, u32[]{:S(2)}, u32[]{:S(2)}) async-start(f32[3,8,10,16,128]{4,3,2,0,1:T(8,128)} %copy.399), calls=%async_computation.3 | async-start | bytes 3932160 | tf_op jit(solution)/shard_map/all_to_all | solution.py:61
  53.1 10.3 %collective-permute-start.2 = (f32[8,10,2,3,128]{4,2,3,1,0:T(2,128)S(1)}, f32[8,10,2,3,128]{4,2,3,1,0:T(2,128)S(1)}, u32[]{:S(2)}, u32[]{:S(2)}) collective-permute-start(f32[8,10,2,3,128]{4,2,3,1,0:T(2,128)S(1)} %get-tuple-element.12), channel_id=1, source_target_pairs={{0,24},{8,0},{16,8},{24,16},{1,25},{9,1},{17,9},{25,17},{2,26},{10... | collective-permute-start | bytes 737288 | tf_op jit(solution)/shard_map/ppermute | solution.py:12
  57.0 11.8 %collective-permute-start.3 = (f32[8,10,2,3,128]{4,2,3,1,0:T(2,128)S(1)}, f32[8,10,2,3,128]{4,2,3,1,0:T(2,128)S(1)}, u32[]{:S(2)}, u32[]{:S(2)}) collective-permute-start(f32[8,10,2,3,128]{4,2,3,1,0:T(2,128)S(1)} %get-tuple-element.13), channel_id=1, source_target_pairs={{0,8},{8,16},{16,24},{24,0},{1,9},{9,17},{17,25},{25,1},{2,10},{10... | collective-permute-start | bytes 737288 | tf_op jit(solution)/shard_map/ppermute | solution.py:12
  83.0 21.5 %collective-permute-start.6 = (f32[8,10,16,128]{3,2,1,0:T(8,128)}, f32[8,10,16,128]{3,2,1,0:T(8,128)}, u32[]{:S(2)}, u32[]{:S(2)}) collective-permute-start(f32[8,10,16,128]{3,2,1,0:T(8,128)} %get-tuple-element.7), channel_id=1, source_target_pairs={{0,24},{8,0},{16,8},{24,16},{1,25},{9,1},{17,9},{25,17},{2,26},{10... | collective-permute-start | bytes 1966088 | tf_op jit(solution)/shard_map/ppermute | solution.py:12
  85.0 29.8 %collective-permute-start.7 = (f32[8,10,16,128]{3,2,1,0:T(8,128)}, f32[8,10,16,128]{3,2,1,0:T(8,128)}, u32[]{:S(2)}, u32[]{:S(2)}) collective-permute-start(f32[8,10,16,128]{3,2,1,0:T(8,128)} %get-tuple-element.8), channel_id=1, source_target_pairs={{0,8},{8,16},{16,24},{24,0},{1,9},{9,17},{17,25},{25,1},{2,10},{10... | collective-permute-start | bytes 1966088 | tf_op jit(solution)/shard_map/ppermute | solution.py:12
  86.1 8.7 %all-to-all-start.6 = ((f32[8,1,810]{2,1,0:T(1,128)}), f32[8,1,810]{2,1,0:T(1,128)S(1)}, u32[]{:S(2)}, u32[]{:S(2)}) async-start(f32[8,1,810]{2,1,0:T(1,128)} %reshape.939), calls=%async_computation.6 | async-start | bytes 57344 | tf_op jit(solution)/shard_map/all_to_all | solution.py:61
  94.7 38.4 %all-to-all-start.2 = ((f32[3,8,10,3,128]{4,3,2,0,1:T(4,128)}), f32[3,8,10,3,128]{4,3,2,0,1:T(4,128)}, u32[]{:S(2)}, u32[]{:S(2)}) async-start(f32[3,8,10,3,128]{4,3,2,0,1:T(4,128)} %copy.393), calls=%async_computation.2 | async-start | bytes 983040 | tf_op jit(solution)/shard_map/all_to_all | solution.py:61
  100.4 36.4 %collective-permute-start.13 = (f32[8,10,27]{2,0,1:T(8,128)S(1)}, f32[8,10,27]{2,0,1:T(8,128)S(1)}, u32[]{:S(2)}, u32[]{:S(2)}) collective-permute-start(f32[8,10,27]{2,0,1:T(8,128)S(1)} %bitcast.222), channel_id=1, source_target_pairs={{0,8},{8,16},{16,24},{24,0},{1,9},{9,17},{17,25},{25,1},{2,10},{10... | collective-permute-start | bytes 25928 | tf_op jit(solution)/shard_map/ppermute | solution.py:12
  102.2 34.5 %collective-permute-start.12 = (f32[8,10,27]{2,0,1:T(8,128)S(1)}, f32[8,10,27]{2,0,1:T(8,128)S(1)}, u32[]{:S(2)}, u32[]{:S(2)}) collective-permute-start(f32[8,10,27]{2,0,1:T(8,128)S(1)} %bitcast.221), channel_id=1, source_target_pairs={{0,24},{8,0},{16,8},{24,16},{1,25},{9,1},{17,9},{25,17},{2,26},{10... | collective-permute-start | bytes 25928 | tf_op jit(solution)/shard_map/ppermute | solution.py:12
  133.1 12.2 %all-to-all-start.4 = ((f32[8,1,12960]{2,1,0:T(1,128)}), f32[8,1,12960]{2,1,0:T(1,128)S(1)}, u32[]{:S(2)}, u32[]{:S(2)}) async-start(f32[8,1,12960]{2,1,0:T(1,128)} %reshape.937), calls=%async_computation.4 | async-start | bytes 835584 | tf_op jit(solution)/shard_map/all_to_all | solution.py:61
  138.0 13.5 %collective-permute-start.4 = (f32[8,10,3,128]{3,2,1,0:T(4,128)S(1)}, f32[8,10,3,128]{3,2,1,0:T(4,128)S(1)}, u32[]{:S(2)}, u32[]{:S(2)}) collective-permute-start(f32[8,10,3,128]{3,2,1,0:T(4,128)S(1)} %get-tuple-element.15), channel_id=1, source_target_pairs={{0,24},{8,0},{16,8},{24,16},{1,25},{9,1},{17,9},{25,17},{2,26},{10... | collective-permute-start | bytes 368648 | tf_op jit(solution)/shard_map/ppermute | solution.py:12
  140.0 11.5 %collective-permute-start.5 = (f32[8,10,3,128]{3,2,1,0:T(4,128)S(1)}, f32[8,10,3,128]{3,2,1,0:T(4,128)S(1)}, u32[]{:S(2)}, u32[]{:S(2)}) collective-permute-start(f32[8,10,3,128]{3,2,1,0:T(4,128)S(1)} %get-tuple-element.16), channel_id=1, source_target_pairs={{0,8},{8,16},{16,24},{24,0},{1,9},{9,17},{17,25},{25,1},{2,10},{10... | collective-permute-start | bytes 368648 | tf_op jit(solution)/shard_map/ppermute | solution.py:12
  149.1 17.1 %collective-permute-start.8 = (f32[8,10,27,16]{2,3,1,0:T(8,128)S(1)}, f32[8,10,27,16]{2,3,1,0:T(8,128)S(1)}, u32[]{:S(2)}, u32[]{:S(2)}) collective-permute-start(f32[8,10,27,16]{2,3,1,0:T(8,128)S(1)} %get-tuple-element.4), channel_id=1, source_target_pairs={{0,24},{8,0},{16,8},{24,16},{1,25},{9,1},{17,9},{25,17},{2,26},{10... | collective-permute-start | bytes 414728 | tf_op jit(solution)/shard_map/ppermute | solution.py:12
  151.1 28.9 %collective-permute-start.9 = (f32[8,10,27,16]{2,3,1,0:T(8,128)S(1)}, f32[8,10,27,16]{2,3,1,0:T(8,128)S(1)}, u32[]{:S(2)}, u32[]{:S(2)}) collective-permute-start(f32[8,10,27,16]{2,3,1,0:T(8,128)S(1)} %get-tuple-element.5), channel_id=1, source_target_pairs={{0,8},{8,16},{16,24},{24,0},{1,9},{9,17},{17,25},{25,1},{2,10},{10... | collective-permute-start | bytes 414728 | tf_op jit(solution)/shard_map/ppermute | solution.py:12
where the time goes:
time: 183 us; the launch traced here: 182 us
  waiting for transfers between devices  62.9 us (34%)
  starting transfers between devices  50.8 us (28%)
  local copies, waits for them, and re-layouts  33.4 us (18%)
  other arithmetic  16.6 us (9%)
  matrix products  16.5 us (9%)
  between operations  2.14 us (1%)
    ppermute x14, waiting for transfers between devices, passed_along(): return lax.ppermute(x, axis, [(i, (i + by) % size) for i in range(size)])  49.3 us
    all_to_all x7, starting transfers between devices, migrate(): lax.all_to_all(shaped, 'rad', split_axis=1, concat_axis=1, tiled=True)  28.8 us
    ppermute x14, starting transfers between devices, passed_along(): return lax.ppermute(x, axis, [(i, (i + by) % size) for i in range(size)])  22 us
    all_to_all x7, waiting for transfers between devices, migrate(): lax.all_to_all(shaped, 'rad', split_axis=1, concat_axis=1, tiled=True)  13.6 us
    gather x12, local copies, waits for them, and re-layouts, arrange(): picked = jnp.take(member, source, axis=0)  10.3 us
    dot_general x1, matrix products, block_sums(): moments = jnp.einsum('snb,sfb->snf', shapes, carried, precision=exact)  8.16 us
    unnamed x18, local copies, waits for them, and re-layouts  8.14 us
    dot_general x2, matrix products, speed(): jnp.einsum('scn,snb->scb', coefficients, basis(points), precision=exact)  6.78 us
  transfers between devices with their start and end apart: 21, of which 10 were waited for; matrix products, arithmetic and copies ran while one was open for 31% of the time, Pallas kernels for 0%

commit v1 on v0

v1 whole, which is shorter than its diff:
```python
import jax
import jax.numpy as jnp
import numpy as np
from jax import lax
from jax.experimental import pallas as pl
from jax.experimental.pallas import tpu as pltpu
from jax.sharding import PartitionSpec as P

time_step = 0.4
exact = lax.Precision.HIGHEST
LANES = 128
VM = pl.BlockSpec(memory_space=pltpu.VMEM)
SM = pl.BlockSpec(memory_space=pltpu.SMEM)
f32 = jnp.float32
bf16 = jnp.bfloat16


def passed_along(x, axis, by):
    size = lax.axis_size(axis)
    return lax.ppermute(x, axis, [(i, (i + by) % size) for i in range(size)])


def lagrange(coord):
    return (
        2.0 * (coord - 0.5) * (coord - 1.0),
        -4.0 * coord * (coord - 1.0),
        2.0 * coord * (coord - 0.5),
    )


def columns_of(velocity, picks):
    owned = velocity.shape[1]
    table = jnp.pad(velocity, ((0, LANES - velocity.shape[0]), (0, 0)))
    chosen = (picks[:, None] == jnp.arange(owned, dtype=jnp.int32)[None, :]).astype(f32)
    return lax.dot_general(chosen, table, (((1,), (1,)), ((), ())), precision=exact)


def eight_speeds(columns, x, y, z):
    lx, ly, lz = lagrange(x), lagrange(y), lagrange(z)
    out = []
    for c in range(3):
        total = None
        for i in range(3):
            plane = None
            for j in range(3):
                base = c * 27 + i * 9 + j * 3
                line = sum(columns[:, base + k : base + k + 1] * lz[k] for k in range(3))
                line = line * ly[j]
                plane = line if plane is None else plane + line
            plane = plane * lx[i]
            total = plane if total is None else total + plane
        out.append(total)
    return out


def midway_kernel(pos_ref, col_ref, out_ref):
    def group(g, carry):
        rows = pl.ds(pl.multiple_of(g * 8, 8), 8)
        x, y, z = (pos_ref[c, rows, :] for c in range(3))
        u = eight_speeds(col_ref[rows, :], x, y, z)
        for c, p in enumerate((x, y, z)):
            out_ref[c, rows, :] = p + (0.5 * time_step) * u[c]
        return carry

    lax.fori_loop(0, pos_ref.shape[1] // 8, group, 0)


def home_kernel(row_ref, src_ref, e2_ref, pos_ref, mid_ref, reply_ref, fields_ref, const_ref,
                out0, out1, out2, cols, land, tiles):
    blocks = pos_ref.shape[1]

    def fetch(g, carry):
        for i in range(8):
            s = g * 8 + i
            cols[pl.ds(s, 1), :] = reply_ref[pl.ds(row_ref[s], 1), :]
        return carry

    lax.fori_loop(0, blocks // 8, fetch, 0)

    def group(g, carry):
        rows = pl.ds(pl.multiple_of(g * 8, 8), 8)
        x, y, z = (mid_ref[c, rows, :] for c in range(3))
        u = eight_speeds(cols[rows, :], x, y, z)
        for c in range(3):
            land[c, rows, :] = pos_ref[c, rows, :] + time_step * u[c]
        return carry

    lax.fori_loop(0, blocks // 8, group, 0)

    lane = lax.broadcasted_iota(jnp.int32, (8, LANES), 1)
    sub = lax.broadcasted_iota(jnp.int32, (8, LANES), 0)
    own_slot = (lane // 16) == sub

    def block(g, carry):
        for i in range(8):
            s = g * 8 + i
            coords = [land[c, pl.ds(s, 1), :] for c in range(3)]
            phi = const_ref[6]
            for c in range(3):
                phi = phi * ((coords[c] - const_ref[2 * c]) * (coords[c] - const_ref[2 * c + 1]))
            high = phi.astype(bf16)
            low = (phi - high.astype(f32)).astype(bf16)
            spread = jnp.concatenate([fields_ref[s]] * 8, axis=0)
            dims = (((1,), (1,)), ((), ()))
            both = lax.dot_general(jnp.concatenate([high, low], axis=0), spread, dims,
                                   preferred_element_type=f32)
            full = both[:32] + both[32:]
            rows = list(coords)
            for j in range(4):
                rows.append(jnp.sum(jnp.where(own_slot, full[8 * j : 8 * j + 8], 0.0), axis=0, keepdims=True))
            weight = jnp.sum(phi * phi, axis=1, keepdims=True)
            tag = (e2_ref[s] + 1).astype(f32)
            last = jnp.where((lane == 32) & (sub == 0), tag, 0.0)
            for j in range(4):
                last = last + jnp.where(lane == sub + 8 * j, weight[8 * j : 8 * j + 8], 0.0)
            rows.append(jnp.sum(last, axis=0, keepdims=True))
            tiles[s] = jnp.concatenate(rows, axis=0)
        return carry

    lax.fori_loop(0, blocks // 8, block, 0)
    tiles[blocks] = jnp.zeros((8, LANES), f32)
    send(src_ref, tiles, (out0, out1, out2))


def send(src_ref, tiles, outs):
    count = outs[0].shape[0]
    step = next(s for s in (8, 4, 2, 1) if count % s == 0)
    for k, out in enumerate(outs):
        def some(g, carry):
            for i in range(step):
                p = g * step + i
                out[p] = tiles[src_ref[k * count + p]]
            return carry

        lax.fori_loop(0, count // step, some, 0)


def middle_kernel(src_ref, in0, in1, in2, out0, out1, out2, tiles):
    count = in0.shape[0]
    for k, ref in enumerate((in0, in1, in2)):
        tiles[k * count : (k + 1) * count] = ref[...]
    tiles[3 * count] = jnp.zeros((8, LANES), f32)
    send(src_ref, tiles, (out0, out1, out2))


def final_kernel(in0, in1, in2, moved_ref, proj_ref):
    count = in0.shape[0]
    owned = proj_ref.shape[2]
    fields = proj_ref.shape[1]
    for k, ref in enumerate((in0, in1, in2)):
        moved_ref[k * count : (k + 1) * count] = ref[:, 0:3, :]

    def row(j):
        return jnp.concatenate([ref[:, j, :] for ref in (in0, in1, in2)], axis=0)

    last = row(7)
    tag = last[:, 32:33].astype(jnp.int32) - 1
    hits = (tag == lax.broadcasted_iota(jnp.int32, (3 * count, owned), 1)).astype(bf16)
    dims = (((0,), (0,)), ((), ()))

    def summed(x):
        high = x.astype(bf16)
        low = (x - high.astype(f32)).astype(bf16)
        return (lax.dot_general(high, hits, dims, preferred_element_type=f32)
                + lax.dot_general(low, hits, dims, preferred_element_type=f32))

    scale = 1.0 / (1.0 + summed(last))
    for j in range(4):
        total = summed(row(3 + j))
        for i in range(8):
            n = 8 * j + i
            if n < proj_ref.shape[0]:
                proj_ref[n] = total[fields * i : fields * (i + 1)] * scale[n : n + 1]


def node_constants():
    roots = ((0.5, 1.0, 2.0), (0.0, 1.0, -4.0), (0.0, 0.5, 2.0))
    table = np.zeros((7, 32, LANES), np.float32)
    for n in range(27):
        table[6, n] = 1.0
        for c, i in enumerate((n // 9, n // 3 % 3, n % 3)):
            table[2 * c, n], table[2 * c + 1, n] = roots[i][0], roots[i][1]
            table[6, n] *= roots[i][2]
    return table


def hop(sheets):
    arrived = []
    for k in (0, 2, 1):
        sheet = lax.all_to_all(sheets[k], "rad", split_axis=0, concat_axis=0, tiled=True)
        if k != 1:
            sheet = passed_along(sheet, "lat", k - 1)
        arrived.append(sheet)
    return arrived[0], arrived[2], arrived[1]


def per_device(positions, fields, velocity, counts, elements, routes):
    lat_count, rad_count = lax.axis_size("lat"), lax.axis_size("rad")
    lat = lax.axis_index("lat")
    devices = lat_count * rad_count
    blocks = positions.shape[0]
    capacity = max(1, 2 * blocks // (3 * rad_count))
    sheet = rad_count * capacity
    places = 3 * sheet
    order = jnp.arange(blocks, dtype=jnp.int32)
    valid = order < counts[0]
    lat_to = (lat + routes[0] // sheet - 1) % lat_count
    row_of = (lat_to * sheet + routes[0] % sheet).astype(jnp.int32)

    at_row = (row_of[None, :] == jnp.arange(devices * capacity, dtype=jnp.int32)[:, None]) & valid[None, :]
    want = jnp.max(jnp.where(at_row, elements[1][None, :], -1), axis=1)
    route = jnp.max(jnp.where(at_row, routes[1][None, :], -1), axis=1)
    request = jnp.concatenate([want.reshape(devices, capacity), route.reshape(devices, capacity)], axis=1)
    request = lax.all_to_all(request, ("lat", "rad"), split_axis=0, concat_axis=0, tiled=True)
    asked, next_route = request[:, :capacity].reshape(-1), request[:, capacity:].reshape(-1)
    reply = columns_of(velocity, asked).reshape(devices, capacity, LANES)
    reply = lax.all_to_all(reply, ("lat", "rad"), split_axis=0, concat_axis=0, tiled=True)
    reply = reply.reshape(devices * capacity, LANES)

    place = jnp.arange(places, dtype=jnp.int32)
    at_place = (routes[0][None, :] == place[:, None]) & valid[None, :]
    first_source = jnp.min(jnp.where(at_place, order[None, :], blocks), axis=1)
    came = jnp.arange(devices * capacity, dtype=jnp.int32)
    sheet_in = (lat - came // sheet + 1) % lat_count
    index_in = sheet_in * sheet + came % sheet
    at_place = next_route[None, :] == place[:, None]
    second_source = jnp.min(jnp.where(at_place, index_in[None, :], places), axis=1)

    points = jnp.transpose(positions, (1, 0, 2))
    midway = pl.pallas_call(
        midway_kernel, out_shape=jax.ShapeDtypeStruct(points.shape, f32),
        in_specs=[VM, VM], out_specs=VM, name="midway",
    )(points, columns_of(velocity, elements[0]))

    part = jax.ShapeDtypeStruct((sheet, 8, LANES), f32)
    sheets = pl.pallas_call(
        home_kernel, out_shape=[part] * 3,
        in_specs=[SM] * 3 + [VM] * 5, out_specs=[VM] * 3, name="home",
        scratch_shapes=[pltpu.VMEM((blocks, LANES), f32), pltpu.VMEM((3, blocks, LANES), f32),
                        pltpu.VMEM((blocks + 1, 8, LANES), f32)],
    )(row_of, first_source, elements[2], points, midway, reply, fields, jnp.asarray(node_constants()))
    sheets = hop(sheets)
    sheets = pl.pallas_call(
        middle_kernel, out_shape=[part] * 3,
        in_specs=[SM] + [VM] * 3, out_specs=[VM] * 3, name="middle",
        scratch_shapes=[pltpu.VMEM((places + 1, 8, LANES), f32)],
    )(second_source, *sheets)
    sheets = hop(sheets)
    return pl.pallas_call(
        final_kernel,
        out_shape=[jax.ShapeDtypeStruct((places,) + positions.shape[1:], f32),
                   jax.ShapeDtypeStruct((27, fields.shape[1], velocity.shape[1]), f32)],
        in_specs=[VM] * 3, out_specs=[VM] * 2, name="final",
    )(*sheets)


def solution(mesh):
    in_specs = (
        P(("lat", "rad"), None, None),
        P(("lat", "rad"), None, None),
        P(None, ("lat", "rad")),
        P(("lat", "rad")),
        P(None, ("lat", "rad")),
        P(None, ("lat", "rad")),
    )
    out_specs = (P(("lat", "rad"), None, None), P(None, None, ("lat", "rad")))

    def body(*args):
        return tuple(per_device(*args))

    return jax.shard_map(
        body, mesh=mesh, in_specs=in_specs, out_specs=out_specs, check_vma=False
    )
```

time: 183 us -> 125 us (0.68)
  blocking collectives: 0 us -> 32.6 us
  waiting for transfers between devices: 62.9 us -> 30.7 us
  local copies, waits for them, and re-layouts: 33.4 us -> 6.53 us
  starting transfers between devices: 50.8 us -> 26 us
  Pallas kernels: 0 us -> 21.6 us
  matrix products: 16.5 us -> 1.24 us
  other arithmetic: 16.6 us -> 4.19 us
    ppermute x14 -> x4, waiting for transfers between devices: 49.3 us -> 0.17 us  [passed_along(): return lax.ppermute(x, axis, [(i, (i + by) % size) for i in range(size)])]
    all_to_all x0 -> x3, blocking collectives: none -> 32.6 us  [hop(): lax.all_to_all(sheets[k], 'rad', split_axis=0, concat_axis=0, tiled=True)]
    pallas_call x0 -> x4, Pallas kernels: none -> 21.6 us  [the longest x1 11.1 us: per_device(): pl.pallas_call(home_kernel, out_shape=[part] * 3, in_specs=[SM] * 3 + [VM...]
    ppermute x14 -> x4, starting transfers between devices: 22 us -> 3.51 us  [passed_along(): return lax.ppermute(x, axis, [(i, (i + by) % size) for i in range(size)])]
    all_to_all x7 -> x5, waiting for transfers between devices: 13.6 us -> 30.6 us  [the longest x3 20 us: hop(): lax.all_to_all(sheets[k], 'rad', split_axis=0, concat_axis=0, tiled=True)]
    dot_general x5 -> x2, matrix products: 16.5 us -> 1.24 us  [columns_of(): lax.dot_general(chosen, table, (((1,), (1,)), ((), ())), precision=exact)]
    gather x14 -> x0, local copies, waits for them, and re-layouts: 11.7 us -> none  [the longest x12 10.3 us: arrange(): picked = jnp.take(member, source, axis=0)]
    all_to_all x7 -> x5, starting transfers between devices: 28.8 us -> 22.4 us  [the longest x3 10.4 us: hop(): lax.all_to_all(sheets[k], 'rad', split_axis=0, concat_axis=0, tiled=True)]
  transfers between devices with their start and end apart: 21 -> 9, of which waited for: 10 -> 6; matrix products, arithmetic and copies ran while one was open for 31% -> 2% of each run, Pallas kernels for 0% -> 4%
where the time goes in v1:
time: 125 us; the launch traced here: 124 us
  blocking collectives  32.6 us (26%)
  waiting for transfers between devices  30.7 us (25%)
  starting transfers between devices  26 us (21%)
  Pallas kernels  21.6 us (17%)
  local copies, waits for them, and re-layouts  6.53 us (5%)
  other arithmetic  4.19 us (3%)
  between operations  1.43 us (1%)
    all_to_all x3, blocking collectives, hop(): lax.all_to_all(sheets[k], 'rad', split_axis=0, concat_axis=0, tiled=True)  32.6 us
    all_to_all x3, waiting for transfers between devices, hop(): lax.all_to_all(sheets[k], 'rad', split_axis=0, concat_axis=0, tiled=True)  20 us
    pallas_call x1, Pallas kernels, per_device(): pl.pallas_call(home_kernel, out_shape=[part] * 3, in_specs=[SM] * 3 + [VM...  11.1 us
    all_to_all x3, starting transfers between devices, hop(): lax.all_to_all(sheets[k], 'rad', split_axis=0, concat_axis=0, tiled=True)  10.4 us
    all_to_all x1, waiting for transfers between devices, per_device(): lax.all_to_all(reply, ('lat', 'rad'), split_axis=0, concat_axis=0, tiled=...  9.38 us
    all_to_all x1, starting transfers between devices, per_device(): lax.all_to_all(request, ('lat', 'rad'), split_axis=0, concat_axis=0, tile...  7.33 us
    pallas_call x1, Pallas kernels, per_device(): pl.pallas_call(midway_kernel, out_shape=jax.ShapeDtypeStruct(points.shape...  5.06 us
    all_to_all x1, starting transfers between devices, per_device(): lax.all_to_all(reply, ('lat', 'rad'), split_axis=0, concat_axis=0, tiled=...  4.69 us
  transfers between devices with their start and end apart: 9, of which 6 were waited for; matrix products, arithmetic and copies ran while one was open for 2% of the time, Pallas kernels for 4%

profile of v1, /device:TPU:0, one launch (start us, length us, event | category | flops | bytes accessed | tf_op | source)
XLA Modules:
  0.0 124.2 jit_solution(16202760628696196115)
XLA Ops:
  1.3 1.4 %slice_bitcast_fusion = (s32[128]{0:T(128)S(1)}, s32[128]{0:T(128)S(1)}, s32[128]{0:T(128)}, s32[128]{0:T(128)S(1)}, s32[128]{0:T(128)S(1)}, /*index=5*/s32[128]{0:T(128)S(1)}) fusion(s32[3,128]{1,0:T(4,128)} %param.11, s32[2,128]{1,0:T(2,128)} %param.12, s32[]{:T(128)S(6)} %axis_index.15), kind=kLoop, calls=%fused_computation.53 | loop fusion | flops 3456 | bytes 5636 | tf_op jit(solution)/shard_map/eq | solution.py:34
  3.1 0.7 pad_add_fusion
  3.8 7.3 %all-to-all-start = ((s32[32,1,20]{2,1,0:T(1,128)}), s32[32,1,20]{2,1,0:T(1,128)S(1)}, u32[]{:S(2)}, u32[]{:S(2)}) async-start(s32[32,1,20]{2,1,0:T(1,128)} %bitcast.5), calls=%async_computation | async-start | bytes 32768 | tf_op jit(solution)/shard_map/all_to_all | solution.py:214
  11.1 0.9 fusion.4.col_ref
  12.0 5.1 %midway.1.mid_ref = f32[3,128,128]{2,1,0:T(8,128)} custom-call(f32[3,128,128]{2,1,0:T(8,128)} %bitcast.21, f32[128,128]{1,0:T(8,128)} %fusion.4.col_ref), custom_call_target="tpu_custom_call" | custom-call | tf_op jit(solution)/shard_map/midway/pallas_call | solution.py:230
  17.1 1.1 all-to-all-done
  18.8 0.7 reshape.59
  19.5 4.7 %all-to-all-start.1 = ((f32[32,10,128]{2,1,0:T(8,128)}), f32[32,10,128]{2,1,0:T(8,128)S(1)}, u32[]{:S(2)}, u32[]{:S(2)}) async-start(f32[32,10,128]{2,1,0:T(8,128)} %reshape.59), calls=%async_computation.1 | async-start | bytes 524288 | tf_op jit(solution)/shard_map/all_to_all | solution.py:217
  24.2 0.7 select_reduce_fusion.3.src_ref
  25.4 9.4 %all-to-all-done.1 = f32[32,10,128]{2,1,0:T(8,128)S(1)} async-done(((f32[32,10,128]{2,1,0:T(8,128)}), f32[32,10,128]{2,1,0:T(8,128)S(1)}, u32[]{:S(2)}, u32[]{:S(2)}) %all-to-all-start.1) | async-done | bytes 163872 | tf_op jit(solution)/shard_map/all_to_all | solution.py:217
  34.8 0.7 reshape.60.reply_ref
  35.4 11.1 %home.1 = (f32[80,8,128]{2,1,0:T(8,128)}, f32[80,8,128]{2,1,0:T(8,128)}, f32[80,8,128]{2,1,0:T(8,128)}) custom-call(s32[128]{0:T(128)} %fusion.21.row_ref, s32[240]{0:T(256)} %select_reduce_fusion.3.src_ref, s32[128]{0:T(128)} %get-tuple-element.28.e2_ref, f32[3,128,128]{2,1,0:T(8,128)} %bitcast.22, f32[3,128,128]{2,1,0:T(8,128)} %midway.1.mid_ref, ...), custom_call_target="tpu_custom_call" | custom-call | tf_op jit(solution)/shard_map/home/pallas_call | solution.py:236
  46.5 10.9 %all_to_all.47 = f32[80,8,128]{2,1,0:T(8,128)S(1)} all-to-all(f32[80,8,128]{2,1,0:T(8,128)} %get-tuple-element.10), channel_id=1, replica_groups=mesh['lat'=4,'rad'=8] {'rad'}, dimensions={0} | all-to-all | bytes 655360 | tf_op jit(solution)/shard_map/all_to_all | solution.py:190
  57.4 3.4 %all-to-all-start.2 = ((f32[80,8,128]{2,1,0:T(8,128)}), f32[80,8,128]{2,1,0:T(8,128)S(1)}, u32[]{:S(2)}, u32[]{:S(2)}) async-start(f32[80,8,128]{2,1,0:T(8,128)} %get-tuple-element.8), calls=%async_computation.2 | async-start | bytes 655360 | tf_op jit(solution)/shard_map/all_to_all | solution.py:190
  60.9 1.0 collective-permute-start.1
  61.9 6.6 %all-to-all-done.2 = f32[80,8,128]{2,1,0:T(8,128)S(1)} async-done(((f32[80,8,128]{2,1,0:T(8,128)}), f32[80,8,128]{2,1,0:T(8,128)S(1)}, u32[]{:S(2)}, u32[]{:S(2)}) %all-to-all-start.2) | async-done | bytes 327712 | tf_op jit(solution)/shard_map/all_to_all | solution.py:190
  68.4 1.3 %collective-permute-start = (f32[80,8,128]{2,1,0:T(8,128)S(1)}, f32[80,8,128]{2,1,0:T(8,128)S(1)}, u32[]{:S(2)}, u32[]{:S(2)}) collective-permute-start(f32[80,8,128]{2,1,0:T(8,128)S(1)} %all-to-all-done.2), channel_id=1, source_target_pairs={{0,24},{8,0},{16,8},{24,16},{1,25},{9,1},{17,9},{25,17},{2,26},{10... | collective-permute-start | bytes 983048 | tf_op jit(solution)/shard_map/ppermute | solution.py:20
  69.8 3.4 %all-to-all-start.3 = ((f32[80,8,128]{2,1,0:T(8,128)}), f32[80,8,128]{2,1,0:T(8,128)S(1)}, u32[]{:S(2)}, u32[]{:S(2)}) async-start(f32[80,8,128]{2,1,0:T(8,128)} %get-tuple-element.9), calls=%async_computation.3 | async-start | bytes 655360 | tf_op jit(solution)/shard_map/all_to_all | solution.py:190
  73.3 0.8 select_reduce_fusion.src_ref
  74.1 6.7 %all-to-all-done.3.in1 = f32[80,8,128]{2,1,0:T(8,128)S(1)} async-done(((f32[80,8,128]{2,1,0:T(8,128)}), f32[80,8,128]{2,1,0:T(8,128)S(1)}, u32[]{:S(2)}, u32[]{:S(2)}) %all-to-all-start.3) | async-done | bytes 327712 | tf_op jit(solution)/shard_map/all_to_all | solution.py:190
  80.8 0.7 copy-done
  81.6 0.7 copy-done.3
  82.3 2.6 %middle.1 = (f32[80,8,128]{2,1,0:T(8,128)}, f32[80,8,128]{2,1,0:T(8,128)}, f32[80,8,128]{2,1,0:T(8,128)}) custom-call(s32[240]{0:T(256)} %select_reduce_fusion.src_ref, f32[80,8,128]{2,1,0:T(8,128)} %copy-done.3, f32[80,8,128]{2,1,0:T(8,128)} %copy-done, f32[80,8,128]{2,1,0:T(8,128)} %copy-done.2), custom_call_target="tpu_custom_call" | custom-call | tf_op jit(solution)/shard_map/middle/pallas_call | solution.py:243
  84.9 10.9 %all_to_all.48 = f32[80,8,128]{2,1,0:T(8,128)S(1)} all-to-all(f32[80,8,128]{2,1,0:T(8,128)} %get-tuple-element.13), channel_id=1, replica_groups=mesh['lat'=4,'rad'=8] {'rad'}, dimensions={0} | all-to-all | bytes 655360 | tf_op jit(solution)/shard_map/all_to_all | solution.py:190
  95.9 3.6 %all-to-all-start.5 = ((f32[80,8,128]{2,1,0:T(8,128)}), f32[80,8,128]{2,1,0:T(8,128)S(1)}, u32[]{:S(2)}, u32[]{:S(2)}) async-start(f32[80,8,128]{2,1,0:T(8,128)} %get-tuple-element.11), calls=%async_computation.5 | async-start | bytes 655360 | tf_op jit(solution)/shard_map/all_to_all | solution.py:190
  99.5 0.8 collective-permute-start.3
  100.2 6.8 %all-to-all-done.5 = f32[80,8,128]{2,1,0:T(8,128)S(1)} async-done(((f32[80,8,128]{2,1,0:T(8,128)}), f32[80,8,128]{2,1,0:T(8,128)S(1)}, u32[]{:S(2)}, u32[]{:S(2)}) %all-to-all-start.5) | async-done | bytes 327712 | tf_op jit(solution)/shard_map/all_to_all | solution.py:190
  107.5 10.7 %all_to_all.49.in1 = f32[80,8,128]{2,1,0:T(8,128)} all-to-all(f32[80,8,128]{2,1,0:T(8,128)S(1)} %copy-done.4), channel_id=1, replica_groups=mesh['lat'=4,'rad'=8] {'rad'}, dimensions={0} | all-to-all | bytes 655360 | tf_op jit(solution)/shard_map/all_to_all | solution.py:190
  118.3 0.6 copy-done.5
  118.9 0.7 copy-done.6
  119.6 2.8 %final.1 = (f32[240,3,128]{2,1,0:T(4,128)}, f32[27,16,256]{2,1,0:T(8,128)}) custom-call(f32[80,8,128]{2,1,0:T(8,128)} %copy-done.6, f32[80,8,128]{2,1,0:T(8,128)} %all_to_all.49.in1, f32[80,8,128]{2,1,0:T(8,128)} %copy-done.5), custom_call_target="tpu_custom_call" | custom-call | tf_op jit(solution)/shard_map/final/pallas_call | solution.py:249
  122.4 1.8 %copy.14 = f32[240,3,128]{2,0,1:T(8,128)} copy(f32[240,3,128]{2,1,0:T(4,128)} %get-tuple-element.20) | data formatting | bytes 737280 | tf_op jit(solution)/shard_map/final/pallas_call | solution.py:249
  (27 shorter events, 2.3 us)
Async XLA Ops:
  0.6 10.5 %copy-start.1 = (f32[81,256]{1,0:T(8,128)S(1)}, f32[81,256]{1,0:T(8,128)}, u32[]{:S(2)}) copy-start(f32[81,256]{1,0:T(8,128)} %param.9) | copy-start | bytes 248836
  3.8 14.4 %all-to-all-start = ((s32[32,1,20]{2,1,0:T(1,128)}), s32[32,1,20]{2,1,0:T(1,128)S(1)}, u32[]{:S(2)}, u32[]{:S(2)}) async-start(s32[32,1,20]{2,1,0:T(1,128)} %bitcast.5), calls=%async_computation | async-start | bytes 32768 | tf_op jit(solution)/shard_map/all_to_all | solution.py:214
  19.5 15.3 %all-to-all-start.1 = ((f32[32,10,128]{2,1,0:T(8,128)}), f32[32,10,128]{2,1,0:T(8,128)S(1)}, u32[]{:S(2)}, u32[]{:S(2)}) async-start(f32[32,10,128]{2,1,0:T(8,128)} %reshape.59), calls=%async_computation.1 | async-start | bytes 524288 | tf_op jit(solution)/shard_map/all_to_all | solution.py:217
  24.2 0.7 copy-start.7
  57.4 11.0 %all-to-all-start.2 = ((f32[80,8,128]{2,1,0:T(8,128)}), f32[80,8,128]{2,1,0:T(8,128)S(1)}, u32[]{:S(2)}, u32[]{:S(2)}) async-start(f32[80,8,128]{2,1,0:T(8,128)} %get-tuple-element.8), calls=%async_computation.2 | async-start | bytes 655360 | tf_op jit(solution)/shard_map/all_to_all | solution.py:190
  60.9 19.9 %collective-permute-start.1 = (f32[80,8,128]{2,1,0:T(8,128)S(1)}, f32[80,8,128]{2,1,0:T(8,128)S(1)}, u32[]{:S(2)}, u32[]{:S(2)}) collective-permute-start(f32[80,8,128]{2,1,0:T(8,128)S(1)} %all_to_all.47), channel_id=1, source_target_pairs={{0,8},{8,16},{16,24},{24,0},{1,9},{9,17},{17,25},{25,1},{2,10},{10... | collective-permute-start | bytes 983048 | tf_op jit(solution)/shard_map/ppermute | solution.py:20
  68.4 12.3 %collective-permute-start = (f32[80,8,128]{2,1,0:T(8,128)S(1)}, f32[80,8,128]{2,1,0:T(8,128)S(1)}, u32[]{:S(2)}, u32[]{:S(2)}) collective-permute-start(f32[80,8,128]{2,1,0:T(8,128)S(1)} %all-to-all-done.2), channel_id=1, source_target_pairs={{0,24},{8,0},{16,8},{24,16},{1,25},{9,1},{17,9},{25,17},{2,26},{10... | collective-permute-start | bytes 983048 | tf_op jit(solution)/shard_map/ppermute | solution.py:20
  69.8 11.0 %all-to-all-start.3 = ((f32[80,8,128]{2,1,0:T(8,128)}), f32[80,8,128]{2,1,0:T(8,128)S(1)}, u32[]{:S(2)}, u32[]{:S(2)}) async-start(f32[80,8,128]{2,1,0:T(8,128)} %get-tuple-element.9), calls=%async_computation.3 | async-start | bytes 655360 | tf_op jit(solution)/shard_map/all_to_all | solution.py:190
  80.7 0.7 copy-start
  80.7 0.8 copy-start.2
  81.6 0.7 copy-start.3
  95.9 11.6 %copy-start.4 = (f32[80,8,128]{2,1,0:T(8,128)S(1)}, f32[80,8,128]{2,1,0:T(8,128)}, u32[]{:S(2)}) copy-start(f32[80,8,128]{2,1,0:T(8,128)} %get-tuple-element.12) | copy-start | bytes 983044
  95.9 11.1 %all-to-all-start.5 = ((f32[80,8,128]{2,1,0:T(8,128)}), f32[80,8,128]{2,1,0:T(8,128)S(1)}, u32[]{:S(2)}, u32[]{:S(2)}) async-start(f32[80,8,128]{2,1,0:T(8,128)} %get-tuple-element.11), calls=%async_computation.5 | async-start | bytes 655360 | tf_op jit(solution)/shard_map/all_to_all | solution.py:190
  99.5 18.7 %collective-permute-start.3 = (f32[80,8,128]{2,1,0:T(8,128)S(1)}, f32[80,8,128]{2,1,0:T(8,128)S(1)}, u32[]{:S(2)}, u32[]{:S(2)}) collective-permute-start(f32[80,8,128]{2,1,0:T(8,128)S(1)} %all_to_all.48), channel_id=1, source_target_pairs={{0,8},{8,16},{16,24},{24,0},{1,9},{9,17},{17,25},{25,1},{2,10},{10... | collective-permute-start | bytes 983048 | tf_op jit(solution)/shard_map/ppermute | solution.py:20
  107.0 11.3 %collective-permute-start.2 = (f32[80,8,128]{2,1,0:T(8,128)S(1)}, f32[80,8,128]{2,1,0:T(8,128)S(1)}, u32[]{:S(2)}, u32[]{:S(2)}) collective-permute-start(f32[80,8,128]{2,1,0:T(8,128)S(1)} %all-to-all-done.5), channel_id=1, source_target_pairs={{0,24},{8,0},{16,8},{24,16},{1,25},{9,1},{17,9},{25,17},{2,26},{10... | collective-permute-start | bytes 983048 | tf_op jit(solution)/shard_map/ppermute | solution.py:20
  118.1 0.7 copy-start.5
  118.9 0.7 copy-start.6

commit v2 on v1

--- a/solution.py
+++ b/solution.py
@@ -1,3 +1,5 @@
+from functools import partial
+
 import jax
 import jax.numpy as jnp
 import numpy as np
@@ -9,6 +11,8 @@
 time_step = 0.4
 exact = lax.Precision.HIGHEST
 LANES = 128
+ROWS = 7
+TAG = 80
 VM = pl.BlockSpec(memory_space=pltpu.VMEM)
 SM = pl.BlockSpec(memory_space=pltpu.SMEM)
 f32 = jnp.float32
@@ -54,19 +58,16 @@
 
 
 def midway_kernel(pos_ref, col_ref, out_ref):
-    def group(g, carry):
-        rows = pl.ds(pl.multiple_of(g * 8, 8), 8)
+    for g in range(pos_ref.shape[1] // 8):
+        rows = slice(g * 8, g * 8 + 8)
         x, y, z = (pos_ref[c, rows, :] for c in range(3))
         u = eight_speeds(col_ref[rows, :], x, y, z)
         for c, p in enumerate((x, y, z)):
             out_ref[c, rows, :] = p + (0.5 * time_step) * u[c]
-        return carry
-
-    lax.fori_loop(0, pos_ref.shape[1] // 8, group, 0)
 
 
 def home_kernel(row_ref, src_ref, e2_ref, pos_ref, mid_ref, reply_ref, fields_ref, const_ref,
-                out0, out1, out2, cols, land, tiles):
+                side, straight, cols, land, tiles, *, capacity):
     blocks = pos_ref.shape[1]
 
     def fetch(g, carry):
@@ -77,19 +78,17 @@
 
     lax.fori_loop(0, blocks // 8, fetch, 0)
 
-    def group(g, carry):
-        rows = pl.ds(pl.multiple_of(g * 8, 8), 8)
+    for g in range(blocks // 8):
+        rows = slice(g * 8, g * 8 + 8)
         x, y, z = (mid_ref[c, rows, :] for c in range(3))
         u = eight_speeds(cols[rows, :], x, y, z)
         for c in range(3):
             land[c, rows, :] = pos_ref[c, rows, :] + time_step * u[c]
-        return carry
-
-    lax.fori_loop(0, blocks // 8, group, 0)
 
     lane = lax.broadcasted_iota(jnp.int32, (8, LANES), 1)
     sub = lax.broadcasted_iota(jnp.int32, (8, LANES), 0)
     own_slot = (lane // 16) == sub
+    tag_slot = (lane == TAG) & (sub == 0)
 
     def block(g, carry):
         for i in range(8):
@@ -105,57 +104,70 @@
             both = lax.dot_general(jnp.concatenate([high, low], axis=0), spread, dims,
                                    preferred_element_type=f32)
             full = both[:32] + both[32:]
-            rows = list(coords)
-            for j in range(4):
-                rows.append(jnp.sum(jnp.where(own_slot, full[8 * j : 8 * j + 8], 0.0), axis=0, keepdims=True))
             weight = jnp.sum(phi * phi, axis=1, keepdims=True)
             tag = (e2_ref[s] + 1).astype(f32)
-            last = jnp.where((lane == 32) & (sub == 0), tag, 0.0)
+            parts = [jnp.where(own_slot, full[8 * j : 8 * j + 8], 0.0) for j in range(4)]
+            parts[3] = jnp.where(tag_slot, tag, parts[3])
             for j in range(4):
-                last = last + jnp.where(lane == sub + 8 * j, weight[8 * j : 8 * j + 8], 0.0)
-            rows.append(jnp.sum(last, axis=0, keepdims=True))
-            tiles[s] = jnp.concatenate(rows, axis=0)
+                parts[3] = jnp.where(lane == sub + (48 + 8 * j), weight[8 * j : 8 * j + 8], parts[3])
+            rows = coords + [jnp.sum(part, axis=0, keepdims=True) for part in parts]
+            tiles[s, 0:7, :] = jnp.concatenate(rows, axis=0)
         return carry
 
     lax.fori_loop(0, blocks // 8, block, 0)
     tiles[blocks] = jnp.zeros((8, LANES), f32)
-    send(src_ref, tiles, (out0, out1, out2))
-
-
-def send(src_ref, tiles, outs):
-    count = outs[0].shape[0]
-    step = next(s for s in (8, 4, 2, 1) if count % s == 0)
-    for k, out in enumerate(outs):
-        def some(g, carry):
-            for i in range(step):
-                p = g * step + i
-                out[p] = tiles[src_ref[k * count + p]]
-            return carry
-
-        lax.fori_loop(0, count // step, some, 0)
-
-
-def middle_kernel(src_ref, in0, in1, in2, out0, out1, out2, tiles):
-    count = in0.shape[0]
-    for k, ref in enumerate((in0, in1, in2)):
-        tiles[k * count : (k + 1) * count] = ref[...]
-    tiles[3 * count] = jnp.zeros((8, LANES), f32)
-    send(src_ref, tiles, (out0, out1, out2))
-
-
-def final_kernel(in0, in1, in2, moved_ref, proj_ref):
-    count = in0.shape[0]
+    send(src_ref, tiles, side, straight, capacity)
+
+
+def send(src_ref, tiles, side, straight, capacity):
+    rad_count = straight.shape[0]
+
+    def some(q, carry):
+        for k in range(3):
+            for c in range(capacity):
+                tile = tiles[src_ref[(k * rad_count + q) * capacity + c], 0:ROWS, :]
+                rows = slice(c * ROWS, (c + 1) * ROWS)
+                if k == 1:
+                    straight[q, rows, :] = tile
+                else:
+                    side[q, k // 2, rows, :] = tile
+        return carry
+
+    lax.fori_loop(0, rad_count, some, 0)
+
+
+def collect(ins, tiles, capacity):
+    rad_count = ins[0].shape[0]
+
+    def some(q, carry):
+        for k, ref in enumerate(ins):
+            for c in range(capacity):
+                p = (k * rad_count + q) * capacity + c
+                tiles[p, 0:ROWS, :] = ref[q, c * ROWS : (c + 1) * ROWS, :]
+        return carry
+
+    lax.fori_loop(0, rad_count, some, 0)
+
+
+def middle_kernel(src_ref, in0, in1, in2, side, straight, tiles, *, capacity):
+    collect((in0, in1, in2), tiles, capacity)
+    tiles[tiles.shape[0] - 1] = jnp.zeros((8, LANES), f32)
+    send(src_ref, tiles, side, straight, capacity)
+
+
+def final_kernel(in0, in1, in2, moved_ref, proj_ref, tiles, *, capacity):
+    places = tiles.shape[0]
     owned = proj_ref.shape[2]
     fields = proj_ref.shape[1]
-    for k, ref in enumerate((in0, in1, in2)):
-        moved_ref[k * count : (k + 1) * count] = ref[:, 0:3, :]
+    collect((in0, in1, in2), tiles, capacity)
+    moved_ref[...] = tiles[:, 0:3, :]
 
     def row(j):
-        return jnp.concatenate([ref[:, j, :] for ref in (in0, in1, in2)], axis=0)
-
-    last = row(7)
-    tag = last[:, 32:33].astype(jnp.int32) - 1
-    hits = (tag == lax.broadcasted_iota(jnp.int32, (3 * count, owned), 1)).astype(bf16)
+        return tiles[:, j, :]
+
+    last = row(6)
+    tag = last[:, TAG : TAG + 1].astype(jnp.int32) - 1
+    hits = (tag == lax.broadcasted_iota(jnp.int32, (places, owned), 1)).astype(bf16)
     dims = (((0,), (0,)), ((), ()))
 
     def summed(x):
@@ -164,9 +176,11 @@
         return (lax.dot_general(high, hits, dims, preferred_element_type=f32)
                 + lax.dot_general(low, hits, dims, preferred_element_type=f32))
 
-    scale = 1.0 / (1.0 + summed(last))
-    for j in range(4):
-        total = summed(row(3 + j))
+    total = summed(last)
+    scale = 1.0 / (1.0 + total[48:80])
+    for j in (3, 0, 1, 2):
+        if j < 3:
+            total = summed(row(3 + j))
         for i in range(8):
             n = 8 * j + i
             if n < proj_ref.shape[0]:
@@ -184,14 +198,12 @@
     return table
 
 
-def hop(sheets):
-    arrived = []
-    for k in (0, 2, 1):
-        sheet = lax.all_to_all(sheets[k], "rad", split_axis=0, concat_axis=0, tiled=True)
-        if k != 1:
-            sheet = passed_along(sheet, "lat", k - 1)
-        arrived.append(sheet)
-    return arrived[0], arrived[2], arrived[1]
+def hop(side, straight):
+    side = lax.all_to_all(side, "rad", split_axis=0, concat_axis=0, tiled=True)
+    back = passed_along(side[:, 0], "lat", -1)
+    onward = passed_along(side[:, 1], "lat", 1)
+    straight = lax.all_to_all(straight, "rad", split_axis=0, concat_axis=0, tiled=True)
+    return back, straight, onward
 
 
 def per_device(positions, fields, velocity, counts, elements, routes):
@@ -232,26 +244,28 @@
         in_specs=[VM, VM], out_specs=VM, name="midway",
     )(points, columns_of(velocity, elements[0]))
 
-    part = jax.ShapeDtypeStruct((sheet, 8, LANES), f32)
-    sheets = pl.pallas_call(
-        home_kernel, out_shape=[part] * 3,
-        in_specs=[SM] * 3 + [VM] * 5, out_specs=[VM] * 3, name="home",
+    group_rows = (ROWS * capacity + 7) // 8 * 8
+    parcels = [jax.ShapeDtypeStruct((rad_count, 2, group_rows, LANES), f32),
+               jax.ShapeDtypeStruct((rad_count, group_rows, LANES), f32)]
+    parcels = pl.pallas_call(
+        partial(home_kernel, capacity=capacity), out_shape=parcels,
+        in_specs=[SM] * 3 + [VM] * 5, out_specs=[VM] * 2, name="home",
         scratch_shapes=[pltpu.VMEM((blocks, LANES), f32), pltpu.VMEM((3, blocks, LANES), f32),
                         pltpu.VMEM((blocks + 1, 8, LANES), f32)],
     )(row_of, first_source, elements[2], points, midway, reply, fields, jnp.asarray(node_constants()))
-    sheets = hop(sheets)
-    sheets = pl.pallas_call(
-        middle_kernel, out_shape=[part] * 3,
-        in_specs=[SM] + [VM] * 3, out_specs=[VM] * 3, name="middle",
+    parcels = pl.pallas_call(
+        partial(middle_kernel, capacity=capacity),
+        out_shape=[jax.ShapeDtypeStruct(x.shape, f32) for x in parcels],
+        in_specs=[SM] + [VM] * 3, out_specs=[VM] * 2, name="middle",
         scratch_shapes=[pltpu.VMEM((places + 1, 8, LANES), f32)],
-    )(second_source, *sheets)
-    sheets = hop(sheets)
+    )(second_source, *hop(*parcels))
     return pl.pallas_call(
-        final_kernel,
+        partial(final_kernel, capacity=capacity),
         out_shape=[jax.ShapeDtypeStruct((places,) + positions.shape[1:], f32),
                    jax.ShapeDtypeStruct((27, fields.shape[1], velocity.shape[1]), f32)],
         in_specs=[VM] * 3, out_specs=[VM] * 2, name="final",
-    )(*sheets)
+        scratch_shapes=[pltpu.VMEM((places, 8, LANES), f32)],
+    )(*hop(*parcels))
 
 
 def solution(mesh):

time: 125 us -> 113 us (0.904)
  waiting for transfers between devices: 30.7 us -> 20.2 us
  blocking collectives: 32.6 us -> 38 us
  starting transfers between devices: 26 us -> 22 us
  Pallas kernels: 21.6 us -> 20.1 us
  local copies, waits for them, and re-layouts: 6.53 us -> 5.2 us
    all_to_all x3 -> x1, waiting for transfers between devices: 20 us -> 6.32 us  [hop(): lax.all_to_all(straight, 'rad', split_axis=0, concat_axis=0, tiled=True)]
    all_to_all x3 -> x1, starting transfers between devices: 10.4 us -> 3.42 us  [hop(): lax.all_to_all(straight, 'rad', split_axis=0, concat_axis=0, tiled=True)]
    all_to_all x3, blocking collectives: 32.6 us -> 38 us  [the longest x2 27.7 us: hop(): side = lax.all_to_all(side, 'rad', split_axis=0, concat_axis=0, tiled=True)]
    ppermute x4, starting transfers between devices: 3.51 us -> 7.75 us  [passed_along(): return lax.ppermute(x, axis, [(i, (i + by) % size) for i in range(size)])]
    ppermute x4, waiting for transfers between devices: 0.17 us -> 2.34 us  [passed_along(): return lax.ppermute(x, axis, [(i, (i + by) % size) for i in range(size)])]
    unnamed x16, local copies, waits for them, and re-layouts: 2.86 us -> 1.45 us
  transfers between devices with their start and end apart: 9 -> 7, of which waited for: 6 -> 5; matrix products, arithmetic and copies ran while one was open for 2% -> 3% of each run, Pallas kernels for 4% -> 4%
where the time goes in v2:
time: 113 us; the launch traced here: 112 us
  blocking collectives  38 us (34%)
  starting transfers between devices  22 us (19%)
  waiting for transfers between devices  20.2 us (18%)
  Pallas kernels  20.1 us (18%)
  local copies, waits for them, and re-layouts  5.2 us (5%)
  other arithmetic  4.27 us (4%)
  between operations  1.42 us (1%)
  matrix products  1.24 us (1%)
    all_to_all x2, blocking collectives, hop(): side = lax.all_to_all(side, 'rad', split_axis=0, concat_axis=0, tiled=True)  27.7 us
    all_to_all x1, blocking collectives, hop(): lax.all_to_all(straight, 'rad', split_axis=0, concat_axis=0, tiled=True)  10.3 us
    pallas_call x1, Pallas kernels, per_device(): pl.pallas_call(partial(home_kernel, capacity=capacity), out_shape=parcels...  9.7 us
    all_to_all x1, waiting for transfers between devices, per_device(): lax.all_to_all(reply, ('lat', 'rad'), split_axis=0, concat_axis=0, tiled=...  9.24 us
    ppermute x4, starting transfers between devices, passed_along(): return lax.ppermute(x, axis, [(i, (i + by) % size) for i in range(size)])  7.75 us
    all_to_all x1, starting transfers between devices, per_device(): lax.all_to_all(request, ('lat', 'rad'), split_axis=0, concat_axis=0, tile...  7.33 us
    all_to_all x1, waiting for transfers between devices, hop(): lax.all_to_all(straight, 'rad', split_axis=0, concat_axis=0, tiled=True)  6.32 us
    pallas_call x1, Pallas kernels, per_device(): pl.pallas_call(midway_kernel, out_shape=jax.ShapeDtypeStruct(points.shape...  3.97 us
  transfers between devices with their start and end apart: 7, of which 5 were waited for; matrix products, arithmetic and copies ran while one was open for 3% of the time, Pallas kernels for 4%

profile of v2, /device:TPU:0, one launch (start us, length us, event | category | flops | bytes accessed | tf_op | source)
XLA Modules:
  0.0 112.5 jit_solution(11789439395743925325)
XLA Ops:
  1.3 1.3 %slice_bitcast_fusion.4 = (s32[128]{0:T(128)S(1)}, s32[128]{0:T(128)S(1)}, s32[128]{0:T(128)}, s32[128]{0:T(128)S(1)}, s32[128]{0:T(128)S(1)}, /*index=5*/s32[128]{0:T(128)S(1)}) fusion(s32[3,128]{1,0:T(4,128)} %param.11, s32[2,128]{1,0:T(2,128)} %param.12, s32[]{:T(128)S(6)} %axis_index.15), kind=kLoop, calls=%fused_computation.57 | loop fusion | flops 3456 | bytes 5636 | tf_op jit(solution)/shard_map/eq | solution.py:38
  2.6 0.2 select_reduce_fusion.2
  3.0 0.7 pad_add_fusion
  3.7 7.3 %all-to-all-start = ((s32[32,1,20]{2,1,0:T(1,128)}), s32[32,1,20]{2,1,0:T(1,128)S(1)}, u32[]{:S(2)}, u32[]{:S(2)}) async-start(s32[32,1,20]{2,1,0:T(1,128)} %bitcast.5), calls=%async_computation | async-start | bytes 32768 | tf_op jit(solution)/shard_map/all_to_all | solution.py:226
  11.1 0.9 fusion.4.col_ref
  12.0 4.0 %midway.1.mid_ref = f32[3,128,128]{2,1,0:T(8,128)} custom-call(f32[3,128,128]{2,1,0:T(8,128)} %bitcast.37, f32[128,128]{1,0:T(8,128)} %fusion.4.col_ref), custom_call_target="tpu_custom_call" | custom-call | tf_op jit(solution)/shard_map/midway/pallas_call | solution.py:242
  15.9 2.3 %all-to-all-done = s32[32,1,20]{2,1,0:T(1,128)S(1)} async-done(((s32[32,1,20]{2,1,0:T(1,128)}), s32[32,1,20]{2,1,0:T(1,128)S(1)}, u32[]{:S(2)}, u32[]{:S(2)}) %all-to-all-start) | async-done | bytes 2592 | tf_op jit(solution)/shard_map/all_to_all | solution.py:226
  18.4 0.3 fusion
  18.8 0.7 reshape.59
  19.5 3.5 %all-to-all-start.1 = ((f32[32,10,128]{2,1,0:T(8,128)}), f32[32,10,128]{2,1,0:T(8,128)S(1)}, u32[]{:S(2)}, u32[]{:S(2)}) async-start(f32[32,10,128]{2,1,0:T(8,128)} %reshape.59), calls=%async_computation.1 | async-start | bytes 524288 | tf_op jit(solution)/shard_map/all_to_all | solution.py:229
  23.0 0.7 select_reduce_fusion.3.src_ref
  23.7 0.6 fusion.21.row_ref
  24.4 9.2 %all-to-all-done.1 = f32[32,10,128]{2,1,0:T(8,128)S(1)} async-done(((f32[32,10,128]{2,1,0:T(8,128)}), f32[32,10,128]{2,1,0:T(8,128)S(1)}, u32[]{:S(2)}, u32[]{:S(2)}) %all-to-all-start.1) | async-done | bytes 163872 | tf_op jit(solution)/shard_map/all_to_all | solution.py:229
  33.6 0.7 reshape.60.reply_ref
  34.3 9.7 %home.1 = (f32[8,2,72,128]{3,2,1,0:T(8,128)}, f32[8,72,128]{2,1,0:T(8,128)}) custom-call(s32[128]{0:T(128)} %fusion.21.row_ref, s32[240]{0:T(256)} %select_reduce_fusion.3.src_ref, s32[128]{0:T(128)} %get-tuple-element.28.e2_ref, f32[3,128,128]{2,1,0:T(8,128)} %bitcast.38, f32[3,128,128]{2,1,0:T(8,128)} %midway.1.mid_ref, f32[320,128]{1,0:T(8,128)} %reshape.60.reply_ref, ...), custom_call_target="tpu_custom_call" | custom-call | tf_op jit(solution)/shard_map/home/pallas_call | solution.py:250
  44.0 13.9 %all_to_all.37 = f32[8,2,72,128]{3,2,1,0:T(8,128)S(1)} all-to-all(f32[8,2,72,128]{3,2,1,0:T(8,128)} %get-tuple-element.6), channel_id=1, replica_groups=mesh['lat'=4,'rad'=8] {'rad'}, dimensions={0} | all-to-all | bytes 1179648 | tf_op jit(solution)/shard_map/all_to_all | solution.py:202
  57.9 1.0 collective-permute-start.1
  58.9 2.9 %collective-permute-start = (f32[8,72,128]{2,1,0:T(8,128)S(1)}, f32[8,72,128]{2,1,0:T(8,128)S(1)}, u32[]{:S(2)}, u32[]{:S(2)}) collective-permute-start(f32[8,72,128]{2,1,0:T(8,128)S(1)} %get-tuple-element.23), channel_id=1, source_target_pairs={{0,24},{8,0},{16,8},{24,16},{1,25},{9,1},{17,9},{25,17},{2,26},{10... | collective-permute-start | bytes 884744 | tf_op jit(solution)/shard_map/ppermute | solution.py:24
  61.8 3.4 %all-to-all-start.3 = ((f32[8,72,128]{2,1,0:T(8,128)}), f32[8,72,128]{2,1,0:T(8,128)S(1)}, u32[]{:S(2)}, u32[]{:S(2)}) async-start(f32[8,72,128]{2,1,0:T(8,128)} %get-tuple-element.7), calls=%async_computation.3 | async-start | bytes 589824 | tf_op jit(solution)/shard_map/all_to_all | solution.py:205
  65.3 0.7 select_reduce_fusion.src_ref
  66.1 6.3 %all-to-all-done.3.in1 = f32[8,72,128]{2,1,0:T(8,128)S(1)} async-done(((f32[8,72,128]{2,1,0:T(8,128)}), f32[8,72,128]{2,1,0:T(8,128)S(1)}, u32[]{:S(2)}, u32[]{:S(2)}) %all-to-all-start.3) | async-done | bytes 294944 | tf_op jit(solution)/shard_map/all_to_all | solution.py:205
  72.4 1.2 %collective-permute-done.in0 = f32[8,72,128]{2,1,0:T(8,128)S(1)} collective-permute-done((f32[8,72,128]{2,1,0:T(8,128)S(1)}, f32[8,72,128]{2,1,0:T(8,128)S(1)}, u32[]{:S(2)}, u32[]{:S(2)}) %collective-permute-start) | collective-permute-done | bytes 294944 | tf_op jit(solution)/shard_map/ppermute | solution.py:24
  73.6 0.7 copy-done.6
  74.3 2.5 %middle.1 = (f32[8,2,72,128]{3,2,1,0:T(8,128)}, f32[8,72,128]{2,1,0:T(8,128)}) custom-call(s32[240]{0:T(256)} %select_reduce_fusion.src_ref, f32[8,72,128]{2,1,0:T(8,128)} %copy-done.6, f32[8,72,128]{2,1,0:T(8,128)} %copy-done, f32[8,72,128]{2,1,0:T(8,128)} %copy-done.5), custom_call_target="tpu_custom_call" | custom-call | tf_op jit(solution)/shard_map/middle/pallas_call | solution.py:256
  76.8 13.9 %all_to_all.38 = f32[8,2,72,128]{3,2,1,0:T(8,128)S(1)} all-to-all(f32[8,2,72,128]{3,2,1,0:T(8,128)} %get-tuple-element.8), channel_id=1, replica_groups=mesh['lat'=4,'rad'=8] {'rad'}, dimensions={0} | all-to-all | bytes 1179648 | tf_op jit(solution)/shard_map/all_to_all | solution.py:202
  90.7 0.4 collective-permute-start.3
  91.1 3.5 %collective-permute-start.2 = (f32[8,72,128]{2,1,0:T(8,128)S(1)}, f32[8,72,128]{2,1,0:T(8,128)S(1)}, u32[]{:S(2)}, u32[]{:S(2)}) collective-permute-start(f32[8,72,128]{2,1,0:T(8,128)S(1)} %get-tuple-element.21), channel_id=1, source_target_pairs={{0,24},{8,0},{16,8},{24,16},{1,25},{9,1},{17,9},{25,17},{2,26},{10... | collective-permute-start | bytes 884744 | tf_op jit(solution)/shard_map/ppermute | solution.py:24
  94.6 10.3 %all_to_all.39.in1 = f32[8,72,128]{2,1,0:T(8,128)} all-to-all(f32[8,72,128]{2,1,0:T(8,128)S(1)} %copy-done.4), channel_id=1, replica_groups=mesh['lat'=4,'rad'=8] {'rad'}, dimensions={0} | all-to-all | bytes 589824 | tf_op jit(solution)/shard_map/all_to_all | solution.py:205
  104.9 1.2 %collective-permute-done.2.in0 = f32[8,72,128]{2,1,0:T(8,128)S(1)} collective-permute-done((f32[8,72,128]{2,1,0:T(8,128)S(1)}, f32[8,72,128]{2,1,0:T(8,128)S(1)}, u32[]{:S(2)}, u32[]{:S(2)}) %collective-permute-start.2) | collective-permute-done | bytes 294944 | tf_op jit(solution)/shard_map/ppermute | solution.py:24
  106.1 0.7 copy-done.3
  106.8 3.9 %final.1 = (f32[240,3,128]{2,1,0:T(4,128)}, f32[27,16,256]{2,1,0:T(8,128)}) custom-call(f32[8,72,128]{2,1,0:T(8,128)} %copy-done.3, f32[8,72,128]{2,1,0:T(8,128)} %all_to_all.39.in1, f32[8,72,128]{2,1,0:T(8,128)} %copy-done.2), custom_call_target="tpu_custom_call" | custom-call | tf_op jit(solution)/shard_map/final/pallas_call | solution.py:262
  110.7 1.8 %copy.26 = f32[240,3,128]{2,0,1:T(8,128)} copy(f32[240,3,128]{2,1,0:T(4,128)} %get-tuple-element.16) | data formatting | bytes 737280 | tf_op jit(solution)/shard_map/final/pallas_call | solution.py:262
  (25 shorter events, 0.6 us)
Async XLA Ops:
  0.6 10.4 %copy-start.1 = (f32[81,256]{1,0:T(8,128)S(1)}, f32[81,256]{1,0:T(8,128)}, u32[]{:S(2)}) copy-start(f32[81,256]{1,0:T(8,128)} %param.9) | copy-start | bytes 248836
  3.7 14.5 %all-to-all-start = ((s32[32,1,20]{2,1,0:T(1,128)}), s32[32,1,20]{2,1,0:T(1,128)S(1)}, u32[]{:S(2)}, u32[]{:S(2)}) async-start(s32[32,1,20]{2,1,0:T(1,128)} %bitcast.5), calls=%async_computation | async-start | bytes 32768 | tf_op jit(solution)/shard_map/all_to_all | solution.py:226
  19.5 14.1 %all-to-all-start.1 = ((f32[32,10,128]{2,1,0:T(8,128)}), f32[32,10,128]{2,1,0:T(8,128)S(1)}, u32[]{:S(2)}, u32[]{:S(2)}) async-start(f32[32,10,128]{2,1,0:T(8,128)} %reshape.59), calls=%async_computation.1 | async-start | bytes 524288 | tf_op jit(solution)/shard_map/all_to_all | solution.py:229
  23.0 0.7 copy-start.7
  57.9 14.5 %collective-permute-start.1 = (f32[8,72,128]{2,1,0:T(8,128)S(1)}, f32[8,72,128]{2,1,0:T(8,128)S(1)}, u32[]{:S(2)}, u32[]{:S(2)}) collective-permute-start(f32[8,72,128]{2,1,0:T(8,128)S(1)} %get-tuple-element.22), channel_id=1, source_target_pairs={{0,8},{8,16},{16,24},{24,0},{1,9},{9,17},{17,25},{25,1},{2,10},{10... | collective-permute-start | bytes 884744 | tf_op jit(solution)/shard_map/ppermute | solution.py:24
  58.9 14.7 %collective-permute-start = (f32[8,72,128]{2,1,0:T(8,128)S(1)}, f32[8,72,128]{2,1,0:T(8,128)S(1)}, u32[]{:S(2)}, u32[]{:S(2)}) collective-permute-start(f32[8,72,128]{2,1,0:T(8,128)S(1)} %get-tuple-element.23), channel_id=1, source_target_pairs={{0,24},{8,0},{16,8},{24,16},{1,25},{9,1},{17,9},{25,17},{2,26},{10... | collective-permute-start | bytes 884744 | tf_op jit(solution)/shard_map/ppermute | solution.py:24
  61.8 10.6 %all-to-all-start.3 = ((f32[8,72,128]{2,1,0:T(8,128)}), f32[8,72,128]{2,1,0:T(8,128)S(1)}, u32[]{:S(2)}, u32[]{:S(2)}) async-start(f32[8,72,128]{2,1,0:T(8,128)} %get-tuple-element.7), calls=%async_computation.3 | async-start | bytes 589824 | tf_op jit(solution)/shard_map/all_to_all | solution.py:205
  72.4 1.2 %copy-start = (f32[8,72,128]{2,1,0:T(8,128)}, f32[8,72,128]{2,1,0:T(8,128)S(1)}, u32[]{:S(2)}) copy-start(f32[8,72,128]{2,1,0:T(8,128)S(1)} %all-to-all-done.3.in1) | copy-start | bytes 884740
  72.4 1.2 %copy-start.5 = (f32[8,72,128]{2,1,0:T(8,128)}, f32[8,72,128]{2,1,0:T(8,128)S(1)}, u32[]{:S(2)}) copy-start(f32[8,72,128]{2,1,0:T(8,128)S(1)} %collective-permute-done.1.in2) | copy-start | bytes 884740
  73.6 0.7 copy-start.6
  90.7 3.9 %copy-start.4 = (f32[8,72,128]{2,1,0:T(8,128)S(1)}, f32[8,72,128]{2,1,0:T(8,128)}, u32[]{:S(2)}) copy-start(f32[8,72,128]{2,1,0:T(8,128)} %get-tuple-element.9) | copy-start | bytes 884740
  90.7 14.2 %collective-permute-start.3 = (f32[8,72,128]{2,1,0:T(8,128)S(1)}, f32[8,72,128]{2,1,0:T(8,128)S(1)}, u32[]{:S(2)}, u32[]{:S(2)}) collective-permute-start(f32[8,72,128]{2,1,0:T(8,128)S(1)} %get-tuple-element.20), channel_id=1, source_target_pairs={{0,8},{8,16},{16,24},{24,0},{1,9},{9,17},{17,25},{25,1},{2,10},{10... | collective-permute-start | bytes 884744 | tf_op jit(solution)/shard_map/ppermute | solution.py:24
  91.1 15.0 %collective-permute-start.2 = (f32[8,72,128]{2,1,0:T(8,128)S(1)}, f32[8,72,128]{2,1,0:T(8,128)S(1)}, u32[]{:S(2)}, u32[]{:S(2)}) collective-permute-start(f32[8,72,128]{2,1,0:T(8,128)S(1)} %get-tuple-element.21), channel_id=1, source_target_pairs={{0,24},{8,0},{16,8},{24,16},{1,25},{9,1},{17,9},{25,17},{2,26},{10... | collective-permute-start | bytes 884744 | tf_op jit(solution)/shard_map/ppermute | solution.py:24
  104.9 1.2 %copy-start.2 = (f32[8,72,128]{2,1,0:T(8,128)}, f32[8,72,128]{2,1,0:T(8,128)S(1)}, u32[]{:S(2)}) copy-start(f32[8,72,128]{2,1,0:T(8,128)S(1)} %collective-permute-done.3.in2) | copy-start | bytes 884740
  106.1 0.7 copy-start.3

commit v3 on v2

--- a/solution.py
+++ b/solution.py
@@ -160,7 +160,8 @@
     owned = proj_ref.shape[2]
     fields = proj_ref.shape[1]
     collect((in0, in1, in2), tiles, capacity)
-    moved_ref[...] = tiles[:, 0:3, :]
+    for c in range(3):
+        moved_ref[c] = tiles[:, c, :]
 
     def row(j):
         return tiles[:, j, :]
@@ -213,28 +214,29 @@
     blocks = positions.shape[0]
     capacity = max(1, 2 * blocks // (3 * rad_count))
     sheet = rad_count * capacity
+    pitch = (capacity + 7) // 8 * 8
     places = 3 * sheet
     order = jnp.arange(blocks, dtype=jnp.int32)
     valid = order < counts[0]
     lat_to = (lat + routes[0] // sheet - 1) % lat_count
-    row_of = (lat_to * sheet + routes[0] % sheet).astype(jnp.int32)
-
-    at_row = (row_of[None, :] == jnp.arange(devices * capacity, dtype=jnp.int32)[:, None]) & valid[None, :]
+    row_of = ((lat_to * rad_count + routes[0] % sheet // capacity) * pitch + routes[0] % capacity).astype(jnp.int32)
+
+    at_row = (row_of[None, :] == jnp.arange(devices * pitch, dtype=jnp.int32)[:, None]) & valid[None, :]
     want = jnp.max(jnp.where(at_row, elements[1][None, :], -1), axis=1)
     route = jnp.max(jnp.where(at_row, routes[1][None, :], -1), axis=1)
-    request = jnp.concatenate([want.reshape(devices, capacity), route.reshape(devices, capacity)], axis=1)
+    request = jnp.concatenate([want.reshape(devices, pitch), route.reshape(devices, pitch)], axis=1)
     request = lax.all_to_all(request, ("lat", "rad"), split_axis=0, concat_axis=0, tiled=True)
-    asked, next_route = request[:, :capacity].reshape(-1), request[:, capacity:].reshape(-1)
-    reply = columns_of(velocity, asked).reshape(devices, capacity, LANES)
+    asked, next_route = request[:, :pitch].reshape(-1), request[:, pitch:].reshape(-1)
+    reply = columns_of(velocity, asked).reshape(devices, pitch, LANES)
     reply = lax.all_to_all(reply, ("lat", "rad"), split_axis=0, concat_axis=0, tiled=True)
-    reply = reply.reshape(devices * capacity, LANES)
+    reply = reply.reshape(devices * pitch, LANES)
 
     place = jnp.arange(places, dtype=jnp.int32)
     at_place = (routes[0][None, :] == place[:, None]) & valid[None, :]
     first_source = jnp.min(jnp.where(at_place, order[None, :], blocks), axis=1)
-    came = jnp.arange(devices * capacity, dtype=jnp.int32)
-    sheet_in = (lat - came // sheet + 1) % lat_count
-    index_in = sheet_in * sheet + came % sheet
+    came = jnp.arange(devices * pitch, dtype=jnp.int32)
+    sheet_in = (lat - came // (rad_count * pitch) + 1) % lat_count
+    index_in = sheet_in * sheet + came // pitch % rad_count * capacity + came % pitch
     at_place = next_route[None, :] == place[:, None]
     second_source = jnp.min(jnp.where(at_place, index_in[None, :], places), axis=1)
 
@@ -259,13 +261,14 @@
         in_specs=[SM] + [VM] * 3, out_specs=[VM] * 2, name="middle",
         scratch_shapes=[pltpu.VMEM((places + 1, 8, LANES), f32)],
     )(second_source, *hop(*parcels))
-    return pl.pallas_call(
+    moved, projected = pl.pallas_call(
         partial(final_kernel, capacity=capacity),
-        out_shape=[jax.ShapeDtypeStruct((places,) + positions.shape[1:], f32),
+        out_shape=[jax.ShapeDtypeStruct((3, places, LANES), f32),
                    jax.ShapeDtypeStruct((27, fields.shape[1], velocity.shape[1]), f32)],
         in_specs=[VM] * 3, out_specs=[VM] * 2, name="final",
         scratch_shapes=[pltpu.VMEM((places, 8, LANES), f32)],
     )(*hop(*parcels))
+    return jnp.transpose(moved, (1, 0, 2)), projected
 
 
 def solution(mesh):

time: 113 us -> 110 us (0.973)
  blocking collectives: 38 us -> 52.3 us
  starting transfers between devices: 22 us -> 13.8 us
  waiting for transfers between devices: 20.2 us -> 13.2 us
  local copies, waits for them, and re-layouts: 5.2 us -> 3.27 us
  other arithmetic: 4.27 us -> 2.88 us
    all_to_all x0 -> x1, blocking collectives: none -> 14.3 us  [per_device(): lax.all_to_all(request, ('lat', 'rad'), split_axis=0, concat_axis=0, tile...]
    all_to_all x1 -> x0, starting transfers between devices: 7.33 us -> none  [per_device(): lax.all_to_all(request, ('lat', 'rad'), split_axis=0, concat_axis=0, tile...]
    all_to_all x1, waiting for transfers between devices: 9.24 us -> 4.45 us  [per_device(): lax.all_to_all(reply, ('lat', 'rad'), split_axis=0, concat_axis=0, tiled=...]
    all_to_all x1 -> x0, waiting for transfers between devices: 2.31 us -> none  [per_device(): lax.all_to_all(request, ('lat', 'rad'), split_axis=0, concat_axis=0, tile...]
    pallas_call x1 -> x0, local copies, waits for them, and re-layouts: 1.79 us -> none  [per_device(): pl.pallas_call(partial(final_kernel, capacity=capacity), out_shape=[jax.S...]
    reshape x4 -> x2, local copies, waits for them, and re-layouts: 1.6 us -> 0.15 us  [the longest x1 0.08 us: per_device(): want.reshape(devices, pitch)]
    unnamed x16 -> x20, local copies, waits for them, and re-layouts: 1.45 us -> 2.81 us
  transfers between devices with their start and end apart: 7 -> 6, of which waited for: 5 -> 4; matrix products, arithmetic and copies ran while one was open for 3% -> 3% of each run, Pallas kernels for 4% -> 4%
where the time goes in v3:
time: 110 us; the launch traced here: 109 us
  blocking collectives  52.3 us (48%)
  Pallas kernels  20.3 us (18%)
  starting transfers between devices  13.8 us (13%)
  waiting for transfers between devices  13.2 us (12%)
  local copies, waits for them, and re-layouts  3.27 us (3%)
  other arithmetic  2.88 us (3%)
  matrix products  2.02 us (2%)
  between operations  1.35 us (1%)
    all_to_all x2, blocking collectives, hop(): side = lax.all_to_all(side, 'rad', split_axis=0, concat_axis=0, tiled=True)  27.7 us
    all_to_all x1, blocking collectives, per_device(): lax.all_to_all(request, ('lat', 'rad'), split_axis=0, concat_axis=0, tile...  14.3 us
    all_to_all x1, blocking collectives, hop(): lax.all_to_all(straight, 'rad', split_axis=0, concat_axis=0, tiled=True)  10.3 us
    pallas_call x1, Pallas kernels, per_device(): pl.pallas_call(partial(home_kernel, capacity=capacity), out_shape=parcels...  9.73 us
    ppermute x4, starting transfers between devices, passed_along(): return lax.ppermute(x, axis, [(i, (i + by) % size) for i in range(size)])  7.75 us
    all_to_all x1, waiting for transfers between devices, hop(): lax.all_to_all(straight, 'rad', split_axis=0, concat_axis=0, tiled=True)  6.37 us
    all_to_all x1, waiting for transfers between devices, per_device(): lax.all_to_all(reply, ('lat', 'rad'), split_axis=0, concat_axis=0, tiled=...  4.45 us
    pallas_call x1, Pallas kernels, per_device(): pl.pallas_call(partial(final_kernel, capacity=capacity), out_shape=[jax.S...  4.01 us
  transfers between devices with their start and end apart: 6, of which 4 were waited for; matrix products, arithmetic and copies ran while one was open for 3% of the time, Pallas kernels for 4%

profile of v3, /device:TPU:0, one launch (start us, length us, event | category | flops | bytes accessed | tf_op | source)
XLA Modules:
  0.0 109.0 jit_solution(531711014420197306)
XLA Ops:
  1.3 0.7 copy-done.8
  2.0 0.6 slice_bitcast_fusion.4
  2.6 0.2 select_reduce_fusion.2
  2.9 0.1 pad_add_fusion
  3.0 14.3 %all_to_all.37 = s32[32,1,32]{2,1,0:T(1,128)S(1)} all-to-all(s32[32,1,32]{2,1,0:T(1,128)S(1)} %bitcast.44), channel_id=1, replica_groups=mesh['lat'=4,'rad'=8] {'lat','rad'}, dimensions={0} | all-to-all | bytes 8192 | tf_op jit(solution)/shard_map/all_to_all | solution.py:228
  17.4 0.1 eq.96
  17.5 1.1 %fusion = f32[512,128]{1,0:T(8,128)} fusion(s32[512]{0:T(512)S(1)} %eq.96, f32[81,256]{1,0:T(8,128)S(1)} %copy-done.2), kind=kOutput, calls=%fused_computation.1 | convolution fusion | flops 201457664 | bytes 347136 | tf_op jit(solution)/shard_map/dot_general | solution.py:39
  18.6 2.6 %all-to-all-start.1 = ((f32[32,16,128]{2,1,0:T(8,128)}), f32[32,16,128]{2,1,0:T(8,128)S(1)}, u32[]{:S(2)}, u32[]{:S(2)}) async-start(f32[32,16,128]{2,1,0:T(8,128)} %bitcast.11), calls=%async_computation.1 | async-start | bytes 524288 | tf_op jit(solution)/shard_map/all_to_all | solution.py:231
  21.2 0.9 fusion.4.col_ref
  22.1 4.0 %midway.1.mid_ref = f32[3,128,128]{2,1,0:T(8,128)} custom-call(f32[3,128,128]{2,1,0:T(8,128)} %bitcast.41, f32[128,128]{1,0:T(8,128)} %fusion.4.col_ref), custom_call_target="tpu_custom_call" | custom-call | tf_op jit(solution)/shard_map/midway/pallas_call | solution.py:244
  26.1 0.7 select_reduce_fusion.3.src_ref
  26.8 0.5 fusion.23.row_ref
  27.3 4.5 %all-to-all-done.1 = f32[32,16,128]{2,1,0:T(8,128)S(1)} async-done(((f32[32,16,128]{2,1,0:T(8,128)}), f32[32,16,128]{2,1,0:T(8,128)S(1)}, u32[]{:S(2)}, u32[]{:S(2)}) %all-to-all-start.1) | async-done | bytes 262176 | tf_op jit(solution)/shard_map/all_to_all | solution.py:231
  31.8 0.7 copy-done.1
  32.5 9.7 %home.1 = (f32[8,2,72,128]{3,2,1,0:T(8,128)}, f32[8,72,128]{2,1,0:T(8,128)}) custom-call(s32[128]{0:T(128)} %fusion.23.row_ref, s32[240]{0:T(256)} %select_reduce_fusion.3.src_ref, s32[128]{0:T(128)} %get-tuple-element.24.e2_ref, f32[3,128,128]{2,1,0:T(8,128)} %bitcast.42, f32[3,128,128]{2,1,0:T(8,128)} %midway.1.mid_ref, f32[512,128]{1,0:T(8,128)} %bitcast.40, ...), custom_call_target="tpu_custom_call" | custom-call | tf_op jit(solution)/shard_map/home/pallas_call | solution.py:252
  42.2 13.9 %all_to_all.38 = f32[8,2,72,128]{3,2,1,0:T(8,128)S(1)} all-to-all(f32[8,2,72,128]{3,2,1,0:T(8,128)} %get-tuple-element.8), channel_id=1, replica_groups=mesh['lat'=4,'rad'=8] {'rad'}, dimensions={0} | all-to-all | bytes 1179648 | tf_op jit(solution)/shard_map/all_to_all | solution.py:203
  56.1 1.0 collective-permute-start.1
  57.1 2.9 %collective-permute-start = (f32[8,72,128]{2,1,0:T(8,128)S(1)}, f32[8,72,128]{2,1,0:T(8,128)S(1)}, u32[]{:S(2)}, u32[]{:S(2)}) collective-permute-start(f32[8,72,128]{2,1,0:T(8,128)S(1)} %get-tuple-element.19), channel_id=1, source_target_pairs={{0,24},{8,0},{16,8},{24,16},{1,25},{9,1},{17,9},{25,17},{2,26},{10... | collective-permute-start | bytes 884744 | tf_op jit(solution)/shard_map/ppermute | solution.py:24
  60.0 3.4 %all-to-all-start.3 = ((f32[8,72,128]{2,1,0:T(8,128)}), f32[8,72,128]{2,1,0:T(8,128)S(1)}, u32[]{:S(2)}, u32[]{:S(2)}) async-start(f32[8,72,128]{2,1,0:T(8,128)} %get-tuple-element.9), calls=%async_computation.3 | async-start | bytes 589824 | tf_op jit(solution)/shard_map/all_to_all | solution.py:206
  63.5 0.1 eq.85
  63.5 0.7 select_reduce_fusion.src_ref
  64.3 6.4 %all-to-all-done.3.in1 = f32[8,72,128]{2,1,0:T(8,128)S(1)} async-done(((f32[8,72,128]{2,1,0:T(8,128)}), f32[8,72,128]{2,1,0:T(8,128)S(1)}, u32[]{:S(2)}, u32[]{:S(2)}) %all-to-all-start.3) | async-done | bytes 294944 | tf_op jit(solution)/shard_map/all_to_all | solution.py:206
  70.6 1.2 %collective-permute-done.in0 = f32[8,72,128]{2,1,0:T(8,128)S(1)} collective-permute-done((f32[8,72,128]{2,1,0:T(8,128)S(1)}, f32[8,72,128]{2,1,0:T(8,128)S(1)}, u32[]{:S(2)}, u32[]{:S(2)}) %collective-permute-start) | collective-permute-done | bytes 294944 | tf_op jit(solution)/shard_map/ppermute | solution.py:24
  71.8 0.7 copy-done.7
  72.5 2.5 %middle.1 = (f32[8,2,72,128]{3,2,1,0:T(8,128)}, f32[8,72,128]{2,1,0:T(8,128)}) custom-call(s32[240]{0:T(256)} %select_reduce_fusion.src_ref, f32[8,72,128]{2,1,0:T(8,128)} %copy-done.7, f32[8,72,128]{2,1,0:T(8,128)} %copy-done, f32[8,72,128]{2,1,0:T(8,128)} %copy-done.6), custom_call_target="tpu_custom_call" | custom-call | tf_op jit(solution)/shard_map/middle/pallas_call | solution.py:258
  75.1 13.9 %all_to_all.39 = f32[8,2,72,128]{3,2,1,0:T(8,128)S(1)} all-to-all(f32[8,2,72,128]{3,2,1,0:T(8,128)} %get-tuple-element.10), channel_id=1, replica_groups=mesh['lat'=4,'rad'=8] {'rad'}, dimensions={0} | all-to-all | bytes 1179648 | tf_op jit(solution)/shard_map/all_to_all | solution.py:203
  89.0 0.4 collective-permute-start.3
  89.4 3.5 %collective-permute-start.2 = (f32[8,72,128]{2,1,0:T(8,128)S(1)}, f32[8,72,128]{2,1,0:T(8,128)S(1)}, u32[]{:S(2)}, u32[]{:S(2)}) collective-permute-start(f32[8,72,128]{2,1,0:T(8,128)S(1)} %get-tuple-element.17), channel_id=1, source_target_pairs={{0,24},{8,0},{16,8},{24,16},{1,25},{9,1},{17,9},{25,17},{2,26},{10... | collective-permute-start | bytes 884744 | tf_op jit(solution)/shard_map/ppermute | solution.py:24
  92.8 10.3 %all_to_all.40.in1 = f32[8,72,128]{2,1,0:T(8,128)} all-to-all(f32[8,72,128]{2,1,0:T(8,128)S(1)} %copy-done.5), channel_id=1, replica_groups=mesh['lat'=4,'rad'=8] {'rad'}, dimensions={0} | all-to-all | bytes 589824 | tf_op jit(solution)/shard_map/all_to_all | solution.py:206
  103.2 1.2 %collective-permute-done.2.in0 = f32[8,72,128]{2,1,0:T(8,128)S(1)} collective-permute-done((f32[8,72,128]{2,1,0:T(8,128)S(1)}, f32[8,72,128]{2,1,0:T(8,128)S(1)}, u32[]{:S(2)}, u32[]{:S(2)}) %collective-permute-start.2) | collective-permute-done | bytes 294944 | tf_op jit(solution)/shard_map/ppermute | solution.py:24
  104.3 0.7 copy-done.4
  105.0 4.0 %final.1 = (f32[3,240,128]{2,1,0:T(8,128)}, f32[27,16,256]{2,1,0:T(8,128)}) custom-call(f32[8,72,128]{2,1,0:T(8,128)} %copy-done.4, f32[8,72,128]{2,1,0:T(8,128)} %all_to_all.40.in1, f32[8,72,128]{2,1,0:T(8,128)} %copy-done.3), custom_call_target="tpu_custom_call" | custom-call | tf_op jit(solution)/shard_map/final/pallas_call | solution.py:264
  (25 shorter events, 0.4 us)
Async XLA Ops:
  1.3 0.7 copy-start.8
  1.3 0.7 copy-start.9
  2.9 14.5 %copy-start.2 = (f32[81,256]{1,0:T(8,128)S(1)}, f32[81,256]{1,0:T(8,128)}, u32[]{:S(2)}) copy-start(f32[81,256]{1,0:T(8,128)} %param.9) | copy-start | bytes 248836
  18.6 13.2 %all-to-all-start.1 = ((f32[32,16,128]{2,1,0:T(8,128)}), f32[32,16,128]{2,1,0:T(8,128)S(1)}, u32[]{:S(2)}, u32[]{:S(2)}) async-start(f32[32,16,128]{2,1,0:T(8,128)} %bitcast.11), calls=%async_computation.1 | async-start | bytes 524288 | tf_op jit(solution)/shard_map/all_to_all | solution.py:231
  31.8 0.7 copy-start.1
  56.1 14.5 %collective-permute-start.1 = (f32[8,72,128]{2,1,0:T(8,128)S(1)}, f32[8,72,128]{2,1,0:T(8,128)S(1)}, u32[]{:S(2)}, u32[]{:S(2)}) collective-permute-start(f32[8,72,128]{2,1,0:T(8,128)S(1)} %get-tuple-element.18), channel_id=1, source_target_pairs={{0,8},{8,16},{16,24},{24,0},{1,9},{9,17},{17,25},{25,1},{2,10},{10... | collective-permute-start | bytes 884744 | tf_op jit(solution)/shard_map/ppermute | solution.py:24
  57.1 14.7 %collective-permute-start = (f32[8,72,128]{2,1,0:T(8,128)S(1)}, f32[8,72,128]{2,1,0:T(8,128)S(1)}, u32[]{:S(2)}, u32[]{:S(2)}) collective-permute-start(f32[8,72,128]{2,1,0:T(8,128)S(1)} %get-tuple-element.19), channel_id=1, source_target_pairs={{0,24},{8,0},{16,8},{24,16},{1,25},{9,1},{17,9},{25,17},{2,26},{10... | collective-permute-start | bytes 884744 | tf_op jit(solution)/shard_map/ppermute | solution.py:24
  60.0 10.6 %all-to-all-start.3 = ((f32[8,72,128]{2,1,0:T(8,128)}), f32[8,72,128]{2,1,0:T(8,128)S(1)}, u32[]{:S(2)}, u32[]{:S(2)}) async-start(f32[8,72,128]{2,1,0:T(8,128)} %get-tuple-element.9), calls=%async_computation.3 | async-start | bytes 589824 | tf_op jit(solution)/shard_map/all_to_all | solution.py:206
  70.6 1.2 %copy-start = (f32[8,72,128]{2,1,0:T(8,128)}, f32[8,72,128]{2,1,0:T(8,128)S(1)}, u32[]{:S(2)}) copy-start(f32[8,72,128]{2,1,0:T(8,128)S(1)} %all-to-all-done.3.in1) | copy-start | bytes 884740
  70.6 1.2 %copy-start.6 = (f32[8,72,128]{2,1,0:T(8,128)}, f32[8,72,128]{2,1,0:T(8,128)S(1)}, u32[]{:S(2)}) copy-start(f32[8,72,128]{2,1,0:T(8,128)S(1)} %collective-permute-done.1.in2) | copy-start | bytes 884740
  71.8 0.7 copy-start.7
  88.9 3.9 %copy-start.5 = (f32[8,72,128]{2,1,0:T(8,128)S(1)}, f32[8,72,128]{2,1,0:T(8,128)}, u32[]{:S(2)}) copy-start(f32[8,72,128]{2,1,0:T(8,128)} %get-tuple-element.11) | copy-start | bytes 884740
  89.0 14.2 %collective-permute-start.3 = (f32[8,72,128]{2,1,0:T(8,128)S(1)}, f32[8,72,128]{2,1,0:T(8,128)S(1)}, u32[]{:S(2)}, u32[]{:S(2)}) collective-permute-start(f32[8,72,128]{2,1,0:T(8,128)S(1)} %get-tuple-element.16), channel_id=1, source_target_pairs={{0,8},{8,16},{16,24},{24,0},{1,9},{9,17},{17,25},{25,1},{2,10},{10... | collective-permute-start | bytes 884744 | tf_op jit(solution)/shard_map/ppermute | solution.py:24
  89.4 15.0 %collective-permute-start.2 = (f32[8,72,128]{2,1,0:T(8,128)S(1)}, f32[8,72,128]{2,1,0:T(8,128)S(1)}, u32[]{:S(2)}, u32[]{:S(2)}) collective-permute-start(f32[8,72,128]{2,1,0:T(8,128)S(1)} %get-tuple-element.17), channel_id=1, source_target_pairs={{0,24},{8,0},{16,8},{24,16},{1,25},{9,1},{17,9},{25,17},{2,26},{10... | collective-permute-start | bytes 884744 | tf_op jit(solution)/shard_map/ppermute | solution.py:24
  103.2 1.2 %copy-start.3 = (f32[8,72,128]{2,1,0:T(8,128)}, f32[8,72,128]{2,1,0:T(8,128)S(1)}, u32[]{:S(2)}) copy-start(f32[8,72,128]{2,1,0:T(8,128)S(1)} %collective-permute-done.3.in2) | copy-start | bytes 884740
  104.3 0.7 copy-start.4

commit v4 on v3

--- a/solution.py
+++ b/solution.py
@@ -90,9 +90,11 @@
     own_slot = (lane // 16) == sub
     tag_slot = (lane == TAG) & (sub == 0)
 
+    step = 16 if blocks % 16 == 0 else 8
+
     def block(g, carry):
-        for i in range(8):
-            s = g * 8 + i
+        for i in range(step):
+            s = g * step + i
             coords = [land[c, pl.ds(s, 1), :] for c in range(3)]
             phi = const_ref[6]
             for c in range(3):
@@ -101,9 +103,9 @@
             low = (phi - high.astype(f32)).astype(bf16)
             spread = jnp.concatenate([fields_ref[s]] * 8, axis=0)
             dims = (((1,), (1,)), ((), ()))
-            both = lax.dot_general(jnp.concatenate([high, low], axis=0), spread, dims,
+            full = lax.dot_general(jnp.concatenate([high, low], axis=1),
+                                   jnp.concatenate([spread, spread], axis=1), dims,
                                    preferred_element_type=f32)
-            full = both[:32] + both[32:]
             weight = jnp.sum(phi * phi, axis=1, keepdims=True)
             tag = (e2_ref[s] + 1).astype(f32)
             parts = [jnp.where(own_slot, full[8 * j : 8 * j + 8], 0.0) for j in range(4)]
@@ -114,7 +116,7 @@
             tiles[s, 0:7, :] = jnp.concatenate(rows, axis=0)
         return carry
 
-    lax.fori_loop(0, blocks // 8, block, 0)
+    lax.fori_loop(0, blocks // step, block, 0)
     tiles[blocks] = jnp.zeros((8, LANES), f32)
     send(src_ref, tiles, side, straight, capacity)
 

time: 110 us -> 109 us (level)
  no operation moved by 1% of the time
where the time goes in v4:
time: 109 us; the launch traced here: 108 us
  blocking collectives  52.3 us (48%)
  Pallas kernels  19.4 us (18%)
  starting transfers between devices  13.8 us (13%)
  waiting for transfers between devices  13.2 us (12%)
  local copies, waits for them, and re-layouts  3.27 us (3%)
  other arithmetic  2.88 us (3%)
  matrix products  2.02 us (2%)
  between operations  1.35 us (1%)
    all_to_all x2, blocking collectives, hop(): side = lax.all_to_all(side, 'rad', split_axis=0, concat_axis=0, tiled=True)  27.7 us
    all_to_all x1, blocking collectives, per_device(): lax.all_to_all(request, ('lat', 'rad'), split_axis=0, concat_axis=0, tile...  14.3 us
    all_to_all x1, blocking collectives, hop(): lax.all_to_all(straight, 'rad', split_axis=0, concat_axis=0, tiled=True)  10.3 us
    pallas_call x1, Pallas kernels, per_device(): pl.pallas_call(partial(home_kernel, capacity=capacity), out_shape=parcels...  8.88 us
    ppermute x4, starting transfers between devices, passed_along(): return lax.ppermute(x, axis, [(i, (i + by) % size) for i in range(size)])  7.75 us
    all_to_all x1, waiting for transfers between devices, hop(): lax.all_to_all(straight, 'rad', split_axis=0, concat_axis=0, tiled=True)  6.37 us
    all_to_all x1, waiting for transfers between devices, per_device(): lax.all_to_all(reply, ('lat', 'rad'), split_axis=0, concat_axis=0, tiled=...  4.45 us
    pallas_call x1, Pallas kernels, per_device(): pl.pallas_call(partial(final_kernel, capacity=capacity), out_shape=[jax.S...  4.01 us
  transfers between devices with their start and end apart: 6, of which 4 were waited for; matrix products, arithmetic and copies ran while one was open for 3% of the time, Pallas kernels for 4%

profile of v4, /device:TPU:0, one launch (start us, length us, event | category | flops | bytes accessed | tf_op | source)
XLA Modules:
  0.0 108.2 jit_solution(8356860149223166435)
XLA Ops:
  1.3 0.7 copy-done.8
  2.0 0.6 slice_bitcast_fusion.4
  2.6 0.2 select_reduce_fusion.2
  2.9 0.1 pad_add_fusion
  3.0 14.3 %all_to_all.37 = s32[32,1,32]{2,1,0:T(1,128)S(1)} all-to-all(s32[32,1,32]{2,1,0:T(1,128)S(1)} %bitcast.44), channel_id=1, replica_groups=mesh['lat'=4,'rad'=8] {'lat','rad'}, dimensions={0} | all-to-all | bytes 8192 | tf_op jit(solution)/shard_map/all_to_all | solution.py:230
  17.4 0.1 eq.96
  17.5 1.1 %fusion = f32[512,128]{1,0:T(8,128)} fusion(s32[512]{0:T(512)S(1)} %eq.96, f32[81,256]{1,0:T(8,128)S(1)} %copy-done.2), kind=kOutput, calls=%fused_computation.1 | convolution fusion | flops 201457664 | bytes 347136 | tf_op jit(solution)/shard_map/dot_general | solution.py:39
  18.6 2.6 %all-to-all-start.1 = ((f32[32,16,128]{2,1,0:T(8,128)}), f32[32,16,128]{2,1,0:T(8,128)S(1)}, u32[]{:S(2)}, u32[]{:S(2)}) async-start(f32[32,16,128]{2,1,0:T(8,128)} %bitcast.11), calls=%async_computation.1 | async-start | bytes 524288 | tf_op jit(solution)/shard_map/all_to_all | solution.py:233
  21.2 0.9 fusion.4.col_ref
  22.1 4.0 %midway.1.mid_ref = f32[3,128,128]{2,1,0:T(8,128)} custom-call(f32[3,128,128]{2,1,0:T(8,128)} %bitcast.41, f32[128,128]{1,0:T(8,128)} %fusion.4.col_ref), custom_call_target="tpu_custom_call" | custom-call | tf_op jit(solution)/shard_map/midway/pallas_call | solution.py:246
  26.1 0.7 select_reduce_fusion.3.src_ref
  26.8 0.5 fusion.23.row_ref
  27.3 4.5 %all-to-all-done.1 = f32[32,16,128]{2,1,0:T(8,128)S(1)} async-done(((f32[32,16,128]{2,1,0:T(8,128)}), f32[32,16,128]{2,1,0:T(8,128)S(1)}, u32[]{:S(2)}, u32[]{:S(2)}) %all-to-all-start.1) | async-done | bytes 262176 | tf_op jit(solution)/shard_map/all_to_all | solution.py:233
  31.8 0.7 copy-done.1
  32.5 8.9 %home.1 = (f32[8,2,72,128]{3,2,1,0:T(8,128)}, f32[8,72,128]{2,1,0:T(8,128)}) custom-call(s32[128]{0:T(128)} %fusion.23.row_ref, s32[240]{0:T(256)} %select_reduce_fusion.3.src_ref, s32[128]{0:T(128)} %get-tuple-element.24.e2_ref, f32[3,128,128]{2,1,0:T(8,128)} %bitcast.42, f32[3,128,128]{2,1,0:T(8,128)} %midway.1.mid_ref, f32[512,128]{1,0:T(8,128)} %bitcast.40, ...), custom_call_target="tpu_custom_call" | custom-call | tf_op jit(solution)/shard_map/home/pallas_call | solution.py:254
  41.4 13.9 %all_to_all.38 = f32[8,2,72,128]{3,2,1,0:T(8,128)S(1)} all-to-all(f32[8,2,72,128]{3,2,1,0:T(8,128)} %get-tuple-element.8), channel_id=1, replica_groups=mesh['lat'=4,'rad'=8] {'rad'}, dimensions={0} | all-to-all | bytes 1179648 | tf_op jit(solution)/shard_map/all_to_all | solution.py:205
  55.3 1.0 collective-permute-start.1
  56.2 2.9 %collective-permute-start = (f32[8,72,128]{2,1,0:T(8,128)S(1)}, f32[8,72,128]{2,1,0:T(8,128)S(1)}, u32[]{:S(2)}, u32[]{:S(2)}) collective-permute-start(f32[8,72,128]{2,1,0:T(8,128)S(1)} %get-tuple-element.19), channel_id=1, source_target_pairs={{0,24},{8,0},{16,8},{24,16},{1,25},{9,1},{17,9},{25,17},{2,26},{10... | collective-permute-start | bytes 884744 | tf_op jit(solution)/shard_map/ppermute | solution.py:24
  59.1 3.4 %all-to-all-start.3 = ((f32[8,72,128]{2,1,0:T(8,128)}), f32[8,72,128]{2,1,0:T(8,128)S(1)}, u32[]{:S(2)}, u32[]{:S(2)}) async-start(f32[8,72,128]{2,1,0:T(8,128)} %get-tuple-element.9), calls=%async_computation.3 | async-start | bytes 589824 | tf_op jit(solution)/shard_map/all_to_all | solution.py:208
  62.6 0.1 eq.85
  62.7 0.7 select_reduce_fusion.src_ref
  63.4 6.4 %all-to-all-done.3.in1 = f32[8,72,128]{2,1,0:T(8,128)S(1)} async-done(((f32[8,72,128]{2,1,0:T(8,128)}), f32[8,72,128]{2,1,0:T(8,128)S(1)}, u32[]{:S(2)}, u32[]{:S(2)}) %all-to-all-start.3) | async-done | bytes 294944 | tf_op jit(solution)/shard_map/all_to_all | solution.py:208
  69.8 1.2 %collective-permute-done.in0 = f32[8,72,128]{2,1,0:T(8,128)S(1)} collective-permute-done((f32[8,72,128]{2,1,0:T(8,128)S(1)}, f32[8,72,128]{2,1,0:T(8,128)S(1)}, u32[]{:S(2)}, u32[]{:S(2)}) %collective-permute-start) | collective-permute-done | bytes 294944 | tf_op jit(solution)/shard_map/ppermute | solution.py:24
  71.0 0.7 copy-done.7
  71.7 2.5 %middle.1 = (f32[8,2,72,128]{3,2,1,0:T(8,128)}, f32[8,72,128]{2,1,0:T(8,128)}) custom-call(s32[240]{0:T(256)} %select_reduce_fusion.src_ref, f32[8,72,128]{2,1,0:T(8,128)} %copy-done.7, f32[8,72,128]{2,1,0:T(8,128)} %copy-done, f32[8,72,128]{2,1,0:T(8,128)} %copy-done.6), custom_call_target="tpu_custom_call" | custom-call | tf_op jit(solution)/shard_map/middle/pallas_call | solution.py:260
  74.2 13.9 %all_to_all.39 = f32[8,2,72,128]{3,2,1,0:T(8,128)S(1)} all-to-all(f32[8,2,72,128]{3,2,1,0:T(8,128)} %get-tuple-element.10), channel_id=1, replica_groups=mesh['lat'=4,'rad'=8] {'rad'}, dimensions={0} | all-to-all | bytes 1179648 | tf_op jit(solution)/shard_map/all_to_all | solution.py:205
  88.1 0.4 collective-permute-start.3
  88.5 3.5 %collective-permute-start.2 = (f32[8,72,128]{2,1,0:T(8,128)S(1)}, f32[8,72,128]{2,1,0:T(8,128)S(1)}, u32[]{:S(2)}, u32[]{:S(2)}) collective-permute-start(f32[8,72,128]{2,1,0:T(8,128)S(1)} %get-tuple-element.17), channel_id=1, source_target_pairs={{0,24},{8,0},{16,8},{24,16},{1,25},{9,1},{17,9},{25,17},{2,26},{10... | collective-permute-start | bytes 884744 | tf_op jit(solution)/shard_map/ppermute | solution.py:24
  92.0 10.3 %all_to_all.40.in1 = f32[8,72,128]{2,1,0:T(8,128)} all-to-all(f32[8,72,128]{2,1,0:T(8,128)S(1)} %copy-done.5), channel_id=1, replica_groups=mesh['lat'=4,'rad'=8] {'rad'}, dimensions={0} | all-to-all | bytes 589824 | tf_op jit(solution)/shard_map/all_to_all | solution.py:208
  102.3 1.2 %collective-permute-done.2.in0 = f32[8,72,128]{2,1,0:T(8,128)S(1)} collective-permute-done((f32[8,72,128]{2,1,0:T(8,128)S(1)}, f32[8,72,128]{2,1,0:T(8,128)S(1)}, u32[]{:S(2)}, u32[]{:S(2)}) %collective-permute-start.2) | collective-permute-done | bytes 294944 | tf_op jit(solution)/shard_map/ppermute | solution.py:24
  103.5 0.7 copy-done.4
  104.2 4.0 %final.1 = (f32[3,240,128]{2,1,0:T(8,128)}, f32[27,16,256]{2,1,0:T(8,128)}) custom-call(f32[8,72,128]{2,1,0:T(8,128)} %copy-done.4, f32[8,72,128]{2,1,0:T(8,128)} %all_to_all.40.in1, f32[8,72,128]{2,1,0:T(8,128)} %copy-done.3), custom_call_target="tpu_custom_call" | custom-call | tf_op jit(solution)/shard_map/final/pallas_call | solution.py:266
  (25 shorter events, 0.4 us)
Async XLA Ops:
  1.3 0.7 copy-start.8
  1.3 0.7 copy-start.9
  2.9 14.5 %copy-start.2 = (f32[81,256]{1,0:T(8,128)S(1)}, f32[81,256]{1,0:T(8,128)}, u32[]{:S(2)}) copy-start(f32[81,256]{1,0:T(8,128)} %param.9) | copy-start | bytes 248836
  18.6 13.2 %all-to-all-start.1 = ((f32[32,16,128]{2,1,0:T(8,128)}), f32[32,16,128]{2,1,0:T(8,128)S(1)}, u32[]{:S(2)}, u32[]{:S(2)}) async-start(f32[32,16,128]{2,1,0:T(8,128)} %bitcast.11), calls=%async_computation.1 | async-start | bytes 524288 | tf_op jit(solution)/shard_map/all_to_all | solution.py:233
  31.8 0.7 copy-start.1
  55.3 14.5 %collective-permute-start.1 = (f32[8,72,128]{2,1,0:T(8,128)S(1)}, f32[8,72,128]{2,1,0:T(8,128)S(1)}, u32[]{:S(2)}, u32[]{:S(2)}) collective-permute-start(f32[8,72,128]{2,1,0:T(8,128)S(1)} %get-tuple-element.18), channel_id=1, source_target_pairs={{0,8},{8,16},{16,24},{24,0},{1,9},{9,17},{17,25},{25,1},{2,10},{10... | collective-permute-start | bytes 884744 | tf_op jit(solution)/shard_map/ppermute | solution.py:24
  56.2 14.7 %collective-permute-start = (f32[8,72,128]{2,1,0:T(8,128)S(1)}, f32[8,72,128]{2,1,0:T(8,128)S(1)}, u32[]{:S(2)}, u32[]{:S(2)}) collective-permute-start(f32[8,72,128]{2,1,0:T(8,128)S(1)} %get-tuple-element.19), channel_id=1, source_target_pairs={{0,24},{8,0},{16,8},{24,16},{1,25},{9,1},{17,9},{25,17},{2,26},{10... | collective-permute-start | bytes 884744 | tf_op jit(solution)/shard_map/ppermute | solution.py:24
  59.1 10.6 %all-to-all-start.3 = ((f32[8,72,128]{2,1,0:T(8,128)}), f32[8,72,128]{2,1,0:T(8,128)S(1)}, u32[]{:S(2)}, u32[]{:S(2)}) async-start(f32[8,72,128]{2,1,0:T(8,128)} %get-tuple-element.9), calls=%async_computation.3 | async-start | bytes 589824 | tf_op jit(solution)/shard_map/all_to_all | solution.py:208
  69.8 1.2 %copy-start = (f32[8,72,128]{2,1,0:T(8,128)}, f32[8,72,128]{2,1,0:T(8,128)S(1)}, u32[]{:S(2)}) copy-start(f32[8,72,128]{2,1,0:T(8,128)S(1)} %all-to-all-done.3.in1) | copy-start | bytes 884740
  69.8 1.2 %copy-start.6 = (f32[8,72,128]{2,1,0:T(8,128)}, f32[8,72,128]{2,1,0:T(8,128)S(1)}, u32[]{:S(2)}) copy-start(f32[8,72,128]{2,1,0:T(8,128)S(1)} %collective-permute-done.1.in2) | copy-start | bytes 884740
  71.0 0.7 copy-start.7
  88.1 3.9 %copy-start.5 = (f32[8,72,128]{2,1,0:T(8,128)S(1)}, f32[8,72,128]{2,1,0:T(8,128)}, u32[]{:S(2)}) copy-start(f32[8,72,128]{2,1,0:T(8,128)} %get-tuple-element.11) | copy-start | bytes 884740
  88.1 14.2 %collective-permute-start.3 = (f32[8,72,128]{2,1,0:T(8,128)S(1)}, f32[8,72,128]{2,1,0:T(8,128)S(1)}, u32[]{:S(2)}, u32[]{:S(2)}) collective-permute-start(f32[8,72,128]{2,1,0:T(8,128)S(1)} %get-tuple-element.16), channel_id=1, source_target_pairs={{0,8},{8,16},{16,24},{24,0},{1,9},{9,17},{17,25},{25,1},{2,10},{10... | collective-permute-start | bytes 884744 | tf_op jit(solution)/shard_map/ppermute | solution.py:24
  88.5 15.0 %collective-permute-start.2 = (f32[8,72,128]{2,1,0:T(8,128)S(1)}, f32[8,72,128]{2,1,0:T(8,128)S(1)}, u32[]{:S(2)}, u32[]{:S(2)}) collective-permute-start(f32[8,72,128]{2,1,0:T(8,128)S(1)} %get-tuple-element.17), channel_id=1, source_target_pairs={{0,24},{8,0},{16,8},{24,16},{1,25},{9,1},{17,9},{25,17},{2,26},{10... | collective-permute-start | bytes 884744 | tf_op jit(solution)/shard_map/ppermute | solution.py:24
  102.3 1.2 %copy-start.3 = (f32[8,72,128]{2,1,0:T(8,128)}, f32[8,72,128]{2,1,0:T(8,128)S(1)}, u32[]{:S(2)}) copy-start(f32[8,72,128]{2,1,0:T(8,128)S(1)} %collective-permute-done.3.in2) | copy-start | bytes 884740
  103.5 0.7 copy-start.4
